TPU v7x, 16 devices: a whole 2x2x2 slice. The times are simulated.
16 devices in a mesh: emb: 2 (over z), col: 2 (over y), row: 4 (over x, core).
Axes of the slice: x: 2, y: 2, z: 2, core: 2. Of those that a mesh axis runs over, the one named last changes fastest.
Arguments:
- inter_mask: int32 [4096, 32768], P('row', 'col')
- emb_user: bfloat16 [4096, 256], P(('row', 'col'), 'emb')
- emb_item: bfloat16 [32768, 256], P(('col', 'row'), 'emb')
- triples: int32 [4096, 3], replicated
Outputs:
- output 1: bfloat16 [4096, 256], P(('row', 'col'), 'emb')
- output 2: bfloat16 [32768, 256], P(('col', 'row'), 'emb')
- output 3: float32 [4096], replicated
All inputs are finite; a program needn't handle non-finite values.
Results may differ from a plain program's by a relative error of at most 0.0133009.
Values are sent between devices in bfloat16 or wider.
A program may use at most 1 GiB of HBM per device.

v0:
```python
import jax
import jax.numpy as jnp
from jax import lax
from jax.sharding import PartitionSpec as P

NUM_LAYERS = 3


def lookup_rows(table, ids, offset):
    own_rows = table.shape[0]
    local_ids = ids - offset
    owned = (local_ids >= 0) & (local_ids < own_rows)
    picked = jnp.take(table, jnp.clip(local_ids, 0, own_rows - 1), axis=0)
    return jnp.where(owned[:, None], picked.astype(jnp.float32), 0.0)


def bpr_terms(final_user, final_item, triples, user_off, item_off):
    num_trip = triples.shape[0]
    fetched = jnp.concatenate([
        lookup_rows(final_user, triples[:, 0], user_off),
        lookup_rows(final_item, triples[:, 1], item_off),
        lookup_rows(final_item, triples[:, 2], item_off)], axis=0)
    fetched = lax.psum(fetched, ("row", "col"))
    e_user = fetched[:num_trip]
    e_pos = fetched[num_trip:2 * num_trip]
    e_neg = fetched[2 * num_trip:]
    score = lax.psum(jnp.sum(e_user * (e_pos - e_neg), axis=1), "emb")
    return jax.nn.softplus(-score)


def norm_adjacency(mask_blk):
    deg_user = lax.psum(jnp.sum(mask_blk, axis=1), "col")
    deg_item = lax.psum(jnp.sum(mask_blk, axis=0), "row")
    inv_user = lax.rsqrt(jnp.maximum(deg_user, 1).astype(jnp.float32))
    inv_item = lax.rsqrt(jnp.maximum(deg_item, 1).astype(jnp.float32))
    return ((inv_user[:, None] * mask_blk.astype(jnp.float32)) * inv_item[None, :]).astype(jnp.bfloat16)


def solution(mesh):
    n_col = mesh.shape["col"]
    n_row = mesh.shape["row"]

    def local_fn(mask_blk, user_sh, item_sh, triples):
        adj_blk = norm_adjacency(mask_blk)
        user_cur = user_sh
        item_cur = item_sh
        user_acc = user_sh.astype(jnp.float32)
        item_acc = item_sh.astype(jnp.float32)
        for layer_idx in range(NUM_LAYERS):
            item_panel = lax.all_gather(item_cur, "row", axis=0, tiled=True)
            user_part = jnp.dot(adj_blk, item_panel, preferred_element_type=jnp.float32)
            user_next = lax.psum_scatter(user_part, "col", scatter_dimension=0, tiled=True).astype(jnp.bfloat16)
            user_panel = lax.all_gather(user_cur, "col", axis=0, tiled=True)
            item_part = lax.dot_general(adj_blk, user_panel, (((0,), (0,)), ((), ())), preferred_element_type=jnp.float32)
            item_next = lax.psum_scatter(item_part, "row", scatter_dimension=0, tiled=True).astype(jnp.bfloat16)
            user_acc = user_acc + user_next.astype(jnp.float32)
            item_acc = item_acc + item_next.astype(jnp.float32)
            user_cur = user_next
            item_cur = item_next
        final_user = (user_acc / (NUM_LAYERS + 1)).astype(jnp.bfloat16)
        final_item = (item_acc / (NUM_LAYERS + 1)).astype(jnp.bfloat16)
        user_off = (lax.axis_index("row") * n_col + lax.axis_index("col")) * final_user.shape[0]
        item_off = (lax.axis_index("col") * n_row + lax.axis_index("row")) * final_item.shape[0]
        return final_user, final_item, bpr_terms(final_user, final_item, triples, user_off, item_off)

    return jax.shard_map(
        local_fn, mesh=mesh,
        in_specs=(P("row", "col"), P(("row", "col"), "emb"), P(("col", "row"), "emb"), P()),
        out_specs=(P(("row", "col"), "emb"), P(("col", "row"), "emb"), P()),
        check_vma=False)
```

profile of v0, /device:TPU:0, one launch (start us, length us, event | category | flops | bytes accessed | tf_op | source)
XLA Modules:
  0.0 600.6 jit_solution(15011481151488676824)
XLA Ops:
  7.2 21.5 %fusion.4 = (s32[1024]{0:T(1024)S(1)}, s32[16384]{0:T(1024)}) fusion(s32[1024,16384]{1,0:T(8,128)} %param.6), kind=kLoop, calls=%fused_computation.33 | loop fusion | flops 33537024 | bytes 67178496 | tf_op jit(solution)/shard_map/reduce_sum | solution.py:32
  29.5 5.5 psum.28
  35.1 5.6 all_gather.19
  40.7 18.7 %all-reduce.3.cloned.1.call-done = s32[16384]{0:T(1024)} async-done(((s32[16384]{0:T(1024)}), s32[16384]{0:T(1024)}) %all-reduce.3.cloned.1.call-update) | async-done | bytes 65552 | tf_op jit(solution)/shard_map/psum | solution.py:33
  60.2 32.9 %multiply_convert_fusion = bf16[1024,16384]{1,0:T(8,128)(2,1)} fusion(s32[1024,16384]{1,0:T(8,128)} %param.6, f32[16384]{0:T(1024)S(1)} %convert_rsqrt_fusion, f32[1024]{0:T(1024)S(1)} %convert_rsqrt_fusion.1), kind=kLoop, calls=%fused_computation.3 | loop fusion | flops 67108864 | bytes 100732928 | tf_op jit(solution)/shard_map/convert_element_type | solution.py:36
  93.2 17.1 %fusion.6 = f32[16384,128]{1,0:T(8,128)} fusion(bf16[1024,16384]{1,0:T(8,128)(2,1)} %multiply_convert_fusion, bf16[1024,128]{1,0:T(8,128)(2,1)S(1)} %all_gather.19), kind=kOutput, calls=%fused_computation.35 | convolution fusion | flops 4294967296 | bytes 42205184 | tf_op jit(solution)/shard_map/dot_general | solution.py:54
  110.3 17.0 %fusion.5 = f32[1024,128]{1,0:T(8,128)} fusion(bf16[1024,16384]{1,0:T(8,128)(2,1)} %multiply_convert_fusion, bf16[16384,128]{1,0:T(8,128)(2,1)} %all-gather.4.cloned.1.call-done), kind=kOutput, calls=%fused_computation.34 | convolution fusion | flops 4294967296 | bytes 38273024 | tf_op jit(solution)/shard_map/dot_general | solution.py:51
  127.4 49.9 %reduce-scatter.9.cloned.1.call-done = f32[4096,128]{1,0:T(8,128)} async-done(((f32[16384,128]{1,0:T(8,128)}), f32[4096,128]{1,0:T(8,128)}) %reduce-scatter.9.cloned.1.call-update) | async-done | bytes 2097168 | tf_op jit(solution)/shard_map/reduce_scatter | solution.py:55
  177.3 2.7 convert_element_type.76
  180.1 12.1 %reduce-scatter.7.cloned.1.call-done = f32[512,128]{1,0:T(8,128)} async-done(((f32[1024,128]{1,0:T(8,128)}), f32[512,128]{1,0:T(8,128)}) %reduce-scatter.7.cloned.1.call-update) | async-done | bytes 262160 | tf_op jit(solution)/shard_map/reduce_scatter | solution.py:52
  193.1 5.8 all_gather.21
  198.9 27.6 %all-gather.6.cloned.1.call-done = bf16[16384,128]{1,0:T(8,128)(2,1)} async-done(((bf16[4096,128]{1,0:T(8,128)(2,1)}), bf16[16384,128]{1,0:T(8,128)(2,1)}) %all-gather.6.cloned.1.call-update) | async-done | bytes 4194320 | tf_op jit(solution)/shard_map/all_gather | solution.py:50
  226.5 16.9 %fusion.7 = f32[1024,128]{1,0:T(8,128)} fusion(bf16[1024,16384]{1,0:T(8,128)(2,1)} %multiply_convert_fusion, bf16[16384,128]{1,0:T(8,128)(2,1)} %all-gather.6.cloned.1.call-done), kind=kOutput, calls=%fused_computation.36 | convolution fusion | flops 4294967296 | bytes 38273024 | tf_op jit(solution)/shard_map/dot_general | solution.py:51
  243.5 17.1 %fusion.8 = f32[16384,128]{1,0:T(8,128)} fusion(bf16[1024,16384]{1,0:T(8,128)(2,1)} %multiply_convert_fusion, bf16[1024,128]{1,0:T(8,128)(2,1)S(1)} %all_gather.21), kind=kOutput, calls=%fused_computation.37 | convolution fusion | flops 4294967296 | bytes 42205184 | tf_op jit(solution)/shard_map/dot_general | solution.py:54
  261.7 6.5 %all_gather.23 = bf16[1024,128]{1,0:T(8,128)(2,1)S(1)} all-gather(bf16[512,128]{1,0:T(8,128)(2,1)S(1)} %convert_element_type.77), channel_id=1, replica_groups=mesh['emb'=2,'col'=2,'row'=4] {'col'}, dimensions={0}, use_global_device_ids=true | all-gather | bytes 393216 | tf_op jit(solution)/shard_map/all_gather | solution.py:53
  268.2 17.1 %fusion.10 = f32[16384,128]{1,0:T(8,128)} fusion(bf16[1024,16384]{1,0:T(8,128)(2,1)} %multiply_convert_fusion, bf16[1024,128]{1,0:T(8,128)(2,1)S(1)} %all_gather.23), kind=kOutput, calls=%fused_computation.39 | convolution fusion | flops 4294967296 | bytes 42205184 | tf_op jit(solution)/shard_map/dot_general | solution.py:54
  285.4 42.3 %reduce-scatter.13.cloned.1.call-done = f32[4096,128]{1,0:T(8,128)} async-done(((f32[16384,128]{1,0:T(8,128)}), f32[4096,128]{1,0:T(8,128)}) %reduce-scatter.13.cloned.1.call-update) | async-done | bytes 2097168 | tf_op jit(solution)/shard_map/reduce_scatter | solution.py:55
  327.7 69.5 %reduce-scatter.17.cloned.1.call-done = f32[4096,128]{1,0:T(8,128)} async-done(((f32[16384,128]{1,0:T(8,128)}), f32[4096,128]{1,0:T(8,128)}) %reduce-scatter.17.cloned.1.call-update) | async-done | bytes 2097168 | tf_op jit(solution)/shard_map/reduce_scatter | solution.py:55
  397.2 4.0 multiply_convert_fusion.1
  402.3 12.1 %gather_fusion.1 = bf16[4096,128]{1,0:T(8,128)(2,1)S(1)} fusion(bf16[4096,128]{1,0:T(8,128)(2,1)S(1)} %get-tuple-element.11, s32[4096]{0:T(1024)S(1)} %fusion.2), kind=kCustom, calls=%fused_computation.clone | custom fusion | bytes 2113536 | tf_op jit(solution)/shard_map/jit(_take)/gather | solution.py:13
  414.4 14.9 %gather_fusion.2 = bf16[4096,128]{1,0:T(8,128)(2,1)} fusion(bf16[4096,128]{1,0:T(8,128)(2,1)S(1)} %get-tuple-element.11, s32[4096]{0:T(1024)S(1)} %fusion.3), kind=kCustom, calls=%fused_computation.1.clone | custom fusion | bytes 2113536 | tf_op jit(solution)/shard_map/jit(_take)/gather | solution.py:13
  429.3 4.4 all-gather.8.cloned.1.call-done
  433.8 16.9 %fusion.9 = f32[1024,128]{1,0:T(8,128)} fusion(bf16[1024,16384]{1,0:T(8,128)(2,1)} %multiply_convert_fusion, bf16[16384,128]{1,0:T(8,128)(2,1)} %all-gather.8.cloned.1.call-done), kind=kOutput, calls=%fused_computation.38 | convolution fusion | flops 4294967296 | bytes 38273024 | tf_op jit(solution)/shard_map/dot_general | solution.py:51
  451.0 7.0 %convert_select_fusion = (f32[4096,128]{1,0:T(8,128)S(1)}, f32[4096,128]{1,0:T(8,128)}) fusion(bf16[4096,128]{1,0:T(8,128)(2,1)} %gather_fusion.2, pred[4096]{0:T(1024)(128)(4,1)S(1)} %compare_and_fusion, pred[4096]{0:T(1024)(128)(4,1)S(1)} %get-tuple-element.14, bf16[4096,128]{1,0:T(8,128)(2,1)S(1)} %gather_fusion.1, ...), kind=kLoop, calls=%fused_computation.8 | loop fusion | flops 3145728 | bytes 6307840 | tf_op jit(solution)/shard_map/jit(_where)/select_n | solution.py:14
  458.0 5.5 reduce-scatter.15.cloned.1.call-done
  463.5 1.1 multiply_convert_fusion.2
  464.7 12.1 %gather_fusion = bf16[4096,128]{1,0:T(8,128)(2,1)S(1)} fusion(bf16[512,128]{1,0:T(8,128)(2,1)S(1)} %multiply_convert_fusion.2, s32[4096]{0:T(1024)S(1)} %broadcast_clamp_fusion), kind=kCustom, calls=%fused_computation.2 | custom fusion | bytes 2113536 | tf_op jit(solution)/shard_map/jit(_take)/gather | solution.py:13
  476.9 1.3 convert_select_fusion.2
  478.5 7.2 %pad_maximum_fusion = f32[12288,128]{1,0:T(8,128)} fusion(f32[4096,128]{1,0:T(8,128)S(1)} %get-tuple-element.18, f32[4096,128]{1,0:T(8,128)S(1)} %copy-done.2, f32[4096,128]{1,0:T(8,128)S(1)} %convert_select_fusion.2), kind=kLoop, calls=%fused_computation.4 | loop fusion | flops 3145728 | bytes 12582912 | tf_op jit(solution)/shard_map/concatenate | solution.py:19
  485.6 96.2 %all-reduce.5.cloned.1.call-done = f32[12288,128]{1,0:T(8,128)} async-done(((f32[12288,128]{1,0:T(8,128)}), f32[12288,128]{1,0:T(8,128)}) %all-reduce.5.cloned.1.call-update) | async-done | bytes 6291472 | tf_op jit(solution)/shard_map/psum | solution.py:23
  581.8 3.5 fusion.1
  585.3 8.1 %psum.31 = f32[4096]{0:T(1024)S(1)} all-reduce(f32[4096]{0:T(1024)S(1)} %fusion.1), channel_id=1, replica_groups=mesh['emb'=2,'col'=2,'row'=4] {'emb'}, use_global_device_ids=true, to_apply=%region_12.14 | all-reduce | flops 4096 | bytes 32768 | tf_op jit(solution)/shard_map/psum | solution.py:27
  (54 shorter events, 6.4 us)
Async XLA Ops:
  7.2 27.9 %copy-start.5 = (bf16[512,128]{1,0:T(8,128)(2,1)S(1)}, bf16[512,128]{1,0:T(8,128)(2,1)}, u32[]{:S(2)}) copy-start(bf16[512,128]{1,0:T(8,128)(2,1)} %param.7) | copy-start | bytes 393220
  7.2 52.2 %all-reduce.3.cloned.1.call-start = ((), (), s32[]{:S(2)}) async-start(), calls=%async_computation.6 | async-start | bytes 131072 | tf_op jit(solution)/shard_map/psum | solution.py:33
  28.7 81.6 %all-gather.4.cloned.1.call-start = ((), (), s32[]{:S(2)}) async-start(), calls=%async_computation.7 | async-start | bytes 5242880 | tf_op jit(solution)/shard_map/all_gather | solution.py:50
  29.5 147.9 %reduce-scatter.9.cloned.1.call-start = ((), (), s32[]{:S(2)}) async-start(), calls=%async_computation.9 | async-start | bytes 10485760 | tf_op jit(solution)/shard_map/reduce_scatter | solution.py:55
  110.3 81.9 %reduce-scatter.7.cloned.1.call-start = ((), (), s32[]{:S(2)}) async-start(), calls=%async_computation.8 | async-start | bytes 786432 | tf_op jit(solution)/shard_map/reduce_scatter | solution.py:52
  127.4 99.2 %all-gather.6.cloned.1.call-start = ((), (), s32[]{:S(2)}) async-start(), calls=%async_computation.10 | async-start | bytes 5242880 | tf_op jit(solution)/shard_map/all_gather | solution.py:50
  180.0 80.7 %reduce-scatter.11.cloned.1.call-start = ((), (), s32[]{:S(2)}) async-start(), calls=%async_computation.11 | async-start | bytes 786432 | tf_op jit(solution)/shard_map/reduce_scatter | solution.py:52
  243.5 84.2 %reduce-scatter.13.cloned.1.call-start = ((), (), s32[]{:S(2)}) async-start(), calls=%async_computation.12 | async-start | bytes 10485760 | tf_op jit(solution)/shard_map/reduce_scatter | solution.py:55
  260.7 136.5 %reduce-scatter.17.cloned.1.call-start = ((), (), s32[]{:S(2)}) async-start(), calls=%async_computation.15 | async-start | bytes 10485760 | tf_op jit(solution)/shard_map/reduce_scatter | solution.py:55
  285.3 111.9 %copy-start.3 = (f32[4096,128]{1,0:T(8,128)S(1)}, f32[4096,128]{1,0:T(8,128)}, u32[]{:S(2)}) copy-start(f32[4096,128]{1,0:T(8,128)} %reduce-scatter.9.cloned.1.call-done) | copy-start | bytes 6291460
  285.4 115.9 %copy-start.6 = (s32[4096,3]{0,1:T(4,128)S(1)}, s32[4096,3]{0,1:T(4,128)}, u32[]{:S(2)}) copy-start(s32[4096,3]{0,1:T(4,128)} %param.9) | copy-start | bytes 147460
  285.4 148.4 %all-gather.8.cloned.1.call-start = ((), (), s32[]{:S(2)}) async-start(), calls=%async_computation.13 | async-start | bytes 5242880 | tf_op jit(solution)/shard_map/all_gather | solution.py:50
  401.2 13.3 %copy-start.1 = (bf16[4096,128]{1,0:T(8,128)(2,1)}, bf16[4096,128]{1,0:T(8,128)(2,1)S(1)}, u32[]{:S(2)}) copy-start(bf16[4096,128]{1,0:T(8,128)(2,1)S(1)} %get-tuple-element.11) | copy-start | bytes 3145732
  401.2 62.3 %reduce-scatter.15.cloned.1.call-start = ((), (), s32[]{:S(2)}) async-start(), calls=%async_computation.14 | async-start | bytes 786432 | tf_op jit(solution)/shard_map/reduce_scatter | solution.py:52
  450.7 12.8 %copy-start.4 = (f32[512,128]{1,0:T(8,128)S(1)}, f32[512,128]{1,0:T(8,128)}, u32[]{:S(2)}) copy-start(f32[512,128]{1,0:T(8,128)} %reduce-scatter.7.cloned.1.call-done) | copy-start | bytes 786436
  450.7 131.1 %all-reduce.5.cloned.1.call-start = ((), (), s32[]{:S(2)}) async-start(), calls=%async_computation.16 | async-start | bytes 12582912 | tf_op jit(solution)/shard_map/psum | solution.py:23
  464.7 12.2 %copy-start = (bf16[512,128]{1,0:T(8,128)(2,1)}, bf16[512,128]{1,0:T(8,128)(2,1)S(1)}, u32[]{:S(2)}) copy-start(bf16[512,128]{1,0:T(8,128)(2,1)S(1)} %multiply_convert_fusion.2) | copy-start | bytes 393220
  464.7 12.2 %copy-start.7 = (pred[4096]{0:T(1024)(128)(4,1)S(1)}, pred[4096]{0:T(1024)(128)(4,1)}, u32[]{:S(2)}) copy-start(pred[4096]{0:T(1024)(128)(4,1)} %get-tuple-element.9) | copy-start | bytes 12292
  464.7 12.2 %copy-start.8 = (pred[4096]{0:T(1024)(128)(4,1)S(1)}, pred[4096]{0:T(1024)(128)(4,1)}, u32[]{:S(2)}) copy-start(pred[4096]{0:T(1024)(128)(4,1)} %get-tuple-element.15) | copy-start | bytes 12292
  476.9 1.6 copy-start.2
Sparse Core Ops, SparseCore 0:
  28.8 30.5 all-reduce.2
  60.9 32.4 all-gather.3
  110.4 66.9 reduce-scatter.8
  179.4 12.6 reduce-scatter.6
  194.1 32.4 all-gather.5
  243.6 12.6 reduce-scatter.10
  260.8 66.8 reduce-scatter.12
  330.3 66.8 reduce-scatter.16
  401.3 32.4 all-gather.7
  450.8 12.6 reduce-scatter.14
  485.8 95.9 all-reduce.4
where the time goes:
time: 601 us
  waiting for transfers between devices  327 us (54%)
  matrix products  102 us (17%)
  other arithmetic  85.4 us (14%)
  local copies, waits for them, and re-layouts  39.5 us (7%)
  blocking collectives  31.6 us (5%)
  between operations  14.1 us (2%)
    reduce_scatter x3, waiting for transfers between devices, local_fn(): lax.psum_scatter(item_part, 'row', scatter_dimension=0, tiled=True)  162 us
    psum x1, waiting for transfers between devices, bpr_terms(): fetched = lax.psum(fetched, ('row', 'col'))  96.2 us
    dot_general x3, matrix products, local_fn(): lax.dot_general(adj_blk, user_panel, (((0,), (0,)), ((), ())), preferred_...  51.3 us
    dot_general x3, matrix products, local_fn(): user_part = jnp.dot(adj_blk, item_panel, preferred_element_type=jnp.float32)  50.9 us
    gather x3, local copies, waits for them, and re-layouts, lookup_rows(): picked = jnp.take(table, jnp.clip(local_ids, 0, own_rows - 1), axis=0)  39.2 us
    convert_element_type x1, other arithmetic, norm_adjacency(): (inv_user[:, None] * mask_blk.astype(jnp.float32) * inv_item[None, :]).as...  32.9 us
    all_gather x3, waiting for transfers between devices, local_fn(): item_panel = lax.all_gather(item_cur, 'row', axis=0, tiled=True)  32.1 us
    reduce_sum x1, other arithmetic, norm_adjacency(): deg_user = lax.psum(jnp.sum(mask_blk, axis=1), 'col')  21.5 us
  transfers between devices with their start and end apart: 11, of which 9 were waited for; matrix products, arithmetic and copies ran while one was open for 24% of the time, Pallas kernels for 0%

commit v1 on v0

v1 whole, which is shorter than its diff:
```python
import functools

import jax
import jax.numpy as jnp
from jax import lax
from jax.experimental import pallas as pl
from jax.experimental.pallas import tpu as pltpu
from jax.sharding import PartitionSpec as P

NUM_LAYERS = 3
F32 = jnp.float32
BF16 = jnp.bfloat16
MESH = pl.DeviceIdType.MESH

CHUNK = 512
MASK_COLS = 512
MASK_SLOTS = 3
SCALE_ROWS = 256
FOLD = 1024


def prop_kernel(mask_hbm, eu_ref, ei_ref, outu_ref, outi_ref,
                adj, mbuf, panel, xsend, xrecv, near, stage, drecv, upanel, upart, yrecv,
                rsum, rscale, csum, ccore, cchip, cfar, rdeg, rdfar,
                msem, ag0_s, ag0_r, deg_s, deg_r, u_s, u_r, y_s, y_r,
                d_s, d_r, x_s, x_r, agx_s, agx_r, agd_s, agd_r, agf_s, agf_r):
    users, items = adj.shape
    own_u = eu_ref.shape[0]
    own_i = ei_ref.shape[0]
    n_chunk = own_i // CHUNK
    row = lax.axis_index("row")
    col = lax.axis_index("col")
    mate = row + 1 - 2 * (row % 2)
    far = (row + 2) % 4
    far_mate = (mate + 2) % 4
    other_col = 1 - col
    to_mate = {"row": mate}
    to_far = {"row": far}
    to_col = {"col": other_col}

    def remote(src, dst, ssem, rsem, target):
        return pltpu.make_async_remote_copy(src_ref=src, dst_ref=dst, send_sem=ssem, recv_sem=rsem,
                                            device_id=target, device_id_type=MESH)

    def rows_of(owner, j, size=CHUNK):
        return pl.ds(pl.multiple_of(owner * own_i + j * size, size), size)

    barrier = pltpu.get_barrier_semaphore()
    for target in (to_mate, to_far, to_col):
        pl.semaphore_signal(barrier, inc=1, device_id=target, device_id_type=MESH)
    pl.semaphore_wait(barrier, 3)

    block = pl.ds(pl.multiple_of(row * own_i, own_i), own_i)
    far_block = pl.ds(pl.multiple_of(far * own_i, own_i), own_i)
    ublock = pl.ds(pl.multiple_of(col * own_u, own_u), own_u)
    oblock = pl.ds(pl.multiple_of(other_col * own_u, own_u), own_u)
    ag0_x = remote(ei_ref, panel.at[0, block], ag0_s.at[0], ag0_r.at[0], to_far)
    ag0_d = remote(ei_ref, panel.at[0, block], ag0_s.at[1], ag0_r.at[1], to_mate)
    ag0_f = remote(panel.at[0, far_block], panel.at[0, far_block], ag0_s.at[2], ag0_r.at[2], to_mate)
    ag0_x.start()
    ag0_d.start()
    u0 = remote(eu_ref, upanel.at[0, ublock], u_s.at[0], u_r.at[0], to_col)
    u0.start()

    n_mask = items // MASK_COLS

    def mask_copy(i):
        cols = pl.ds(pl.multiple_of(i * MASK_COLS, MASK_COLS), MASK_COLS)
        slot = i % MASK_SLOTS
        return pltpu.make_async_copy(mask_hbm.at[:, cols], mbuf.at[slot], msem.at[slot])

    for i in range(MASK_SLOTS - 1):
        mask_copy(i).start()
    panel[0, block, :] = ei_ref[...]
    upanel[0, ublock, :] = eu_ref[...]
    rsum[...] = jnp.zeros_like(rsum)

    def mask_step(i, carry):
        mask_copy(i).wait()

        @pl.when(i + MASK_SLOTS - 1 < n_mask)
        def _():
            mask_copy(i + MASK_SLOTS - 1).start()

        cols = pl.ds(pl.multiple_of(i * MASK_COLS, MASK_COLS), MASK_COLS)
        slot = i % MASK_SLOTS

        def tile(t, acc):
            rows = pl.ds(pl.multiple_of(t * 64, 64), 64)
            m = mbuf[slot, rows, :].astype(F32)
            adj[rows, cols] = m.astype(BF16)
            part = m[:, 0:128]
            for g in range(1, MASK_COLS // 128):
                part = part + m[:, g * 128:(g + 1) * 128]
            rsum[rows, :] += part
            return acc + jnp.sum(m.reshape(8, 8, MASK_COLS), axis=0)

        acc = lax.fori_loop(0, users // 64, tile, jnp.zeros((8, MASK_COLS), F32))
        csum[:, cols] = jnp.sum(acc, axis=0, keepdims=True)
        return carry

    lax.fori_loop(0, n_mask, mask_step, 0)

    deg_d = remote(csum, ccore, deg_s.at[0], deg_r.at[0], to_mate)
    deg_d.start()
    ones = jnp.ones((8, 128), BF16)
    rdeg[...] = lax.dot_general(ones, rsum[...].astype(BF16), (((1,), (1,)), ((), ())),
                                preferred_element_type=F32)
    deg_y = remote(rdeg, rdfar, deg_s.at[1], deg_r.at[1], to_col)
    deg_y.start()
    deg_d.wait()
    cchip[...] = csum[...] + ccore[...]
    deg_x = remote(cchip, cfar, deg_s.at[2], deg_r.at[2], to_far)
    deg_x.start()
    ag0_x.wait_recv()
    ag0_f.start()
    u0.wait_recv()
    deg_y.wait()
    deg_u = jnp.maximum(rdeg[0:1, :] + rdfar[0:1, :], 1.0)
    rscale[...] = lax.rsqrt(jnp.broadcast_to(deg_u, (128, users)).T)
    deg_x.wait()
    csum[...] = lax.rsqrt(jnp.maximum(cchip[...] + cfar[...], 1.0))

    def scale_block(owner, j):
        cols = rows_of(owner, j)
        ci = csum[:, cols]

        def tile(t, carry):
            rows = pl.ds(pl.multiple_of(t * SCALE_ROWS, SCALE_ROWS), SCALE_ROWS)
            ru = rscale[rows, :]
            for g in range(CHUNK // 128):
                sub = pl.ds(pl.multiple_of(owner * own_i + j * CHUNK + g * 128, 128), 128)
                m = adj[rows, sub].astype(F32)
                adj[rows, sub] = ((ru * m) * ci[:, g * 128:(g + 1) * 128]).astype(BF16)
            return carry

        lax.fori_loop(0, users // SCALE_ROWS, tile, 0)

    def item_part(owner, j, layer):
        return lax.dot_general(adj[:, rows_of(owner, j)], upanel[layer - 1], (((0,), (0,)), ((), ())),
                               preferred_element_type=F32)

    def core_copy(slot):
        return remote(stage.at[slot], drecv.at[slot], d_s.at[slot], d_r.at[slot], to_mate)

    def chunk_rows(j):
        return pl.ds(pl.multiple_of(j * CHUNK, CHUNK), CHUNK)

    def x_copy(j, layer):
        par = layer % 2
        return remote(xsend.at[chunk_rows(j)], xrecv.at[par, chunk_rows(j)], x_s.at[j], x_r.at[par, j], to_far)

    def item_send_step(j, layer):
        slot = j % 2
        if layer == 1:
            @pl.when(j >= 2)
            def _():
                core_copy(slot).wait_send()
            scale_block(far_mate, j)
            scale_block(mate, j)
        else:
            core_copy(slot).wait_send()
        stage[slot, 0:CHUNK, :] = item_part(far_mate, j, layer)
        stage[slot, CHUNK:2 * CHUNK, :] = item_part(mate, j, layer)
        core_copy(slot).start()
        if layer == 1:
            scale_block(far, j)
            scale_block(row, j)
        else:
            x_copy(j, layer - 1).wait_send()
        xsend[chunk_rows(j), :] = item_part(far, j, layer)
        near[chunk_rows(j), :] = item_part(row, j, layer)
        core_copy(slot).wait_recv()
        xsend[chunk_rows(j), :] += drecv[slot, 0:CHUNK, :]
        near[chunk_rows(j), :] += drecv[slot, CHUNK:2 * CHUNK, :]
        x_copy(j, layer).start()

    def ag_copy(kind, j, layer):
        par = layer % 2
        block = panel.at[par, rows_of(far if kind == "fwd" else row, j)]
        ssem, rsem, target = {"x": (agx_s, agx_r, to_far), "mate": (agd_s, agd_r, to_mate),
                              "fwd": (agf_s, agf_r, to_mate)}[kind]
        return remote(block, block, ssem.at[j], rsem.at[par, j], target)

    def finish_item(j, layer):
        x_copy(j, layer).wait_recv()
        par = layer % 2
        value = (near[chunk_rows(j), :] + xrecv[par, chunk_rows(j), :]).astype(BF16)
        if layer < NUM_LAYERS:
            panel[par, rows_of(row, j), :] = value
            ag_copy("x", j, layer).start()
            ag_copy("mate", j, layer).start()
        else:
            total = ei_ref[chunk_rows(j), :].astype(F32) + panel[1, rows_of(row, j), :].astype(F32)
            total = total + panel[0, rows_of(row, j), :].astype(F32)
            total = total + value.astype(F32)
            outi_ref[chunk_rows(j), :] = (total / (NUM_LAYERS + 1)).astype(BF16)

    def gather_items(layer):
        def forward(j, carry):
            ag_copy("x", j, layer).wait_recv()
            ag_copy("fwd", j, layer).start()
            return carry

        def settle(j, carry):
            ag_copy("mate", j, layer).wait_recv()
            ag_copy("fwd", j, layer).wait_recv()
            for kind in ("x", "mate", "fwd"):
                ag_copy(kind, j, layer).wait_send()
            return carry

        lax.fori_loop(0, n_chunk, forward, 0)
        lax.fori_loop(0, n_chunk, settle, 0)

    def user_part(layer):
        par = (layer - 1) % 2
        upart[...] = jnp.zeros_like(upart)

        def fold(i, carry):
            cols = pl.ds(pl.multiple_of(i * FOLD, FOLD), FOLD)
            upart[...] += jnp.dot(adj[:, cols], panel[par, cols, :], preferred_element_type=F32)
            return carry

        lax.fori_loop(0, items // FOLD, fold, 0)

    def y_copy(layer):
        return remote(upart.at[oblock], yrecv.at[layer - 1], y_s.at[layer - 1], y_r.at[layer - 1], to_col)

    def u_copy(layer):
        return remote(upanel.at[layer, ublock], upanel.at[layer, ublock], u_s.at[layer], u_r.at[layer], to_col)

    def finish_user(layer):
        y_copy(layer).wait()
        value = (upart[ublock, :] + yrecv[layer - 1]).astype(BF16)
        if layer < NUM_LAYERS:
            upanel[layer, ublock, :] = value
            u_copy(layer).start()
        else:
            total = eu_ref[...].astype(F32) + upanel[1, ublock, :].astype(F32)
            total = total + upanel[2, ublock, :].astype(F32)
            total = total + value.astype(F32)
            outu_ref[...] = (total / (NUM_LAYERS + 1)).astype(BF16)

    def loop(lo, hi, body):
        def step(j, carry):
            body(j)
            return carry
        lax.fori_loop(lo, hi, step, 0)

    for layer in range(1, NUM_LAYERS + 1):
        loop(0, n_chunk, functools.partial(item_send_step, layer=layer))
        if layer == 1:
            ag0_d.wait_recv()
            ag0_f.wait_recv()
            ag0_x.wait_send()
            ag0_d.wait_send()
            ag0_f.wait_send()
            u0.wait_send()
        else:
            gather_items(layer - 1)
        user_part(layer)
        y_copy(layer).start()
        loop(0, n_chunk // 2, functools.partial(finish_item, layer=layer))
        finish_user(layer)
        loop(n_chunk // 2, n_chunk, functools.partial(finish_item, layer=layer))
        if layer < NUM_LAYERS:
            u_copy(layer).wait()

    for slot in range(2):
        core_copy(slot).wait_send()
    for j in range(n_chunk):
        x_copy(j, NUM_LAYERS).wait_send()


def propagate(mask_blk, user_sh, item_sh):
    users, items = mask_blk.shape
    own_u, dim = user_sh.shape
    own_i = item_sh.shape[0]
    n_chunk = own_i // CHUNK
    vmem, dma = pltpu.VMEM, pltpu.SemaphoreType.DMA
    return pl.pallas_call(
        prop_kernel,
        name="propagate",
        out_shape=(jax.ShapeDtypeStruct((own_u, dim), BF16), jax.ShapeDtypeStruct((own_i, dim), BF16)),
        in_specs=[pl.BlockSpec(memory_space=pl.ANY), pl.BlockSpec(memory_space=pltpu.VMEM),
                  pl.BlockSpec(memory_space=pltpu.VMEM)],
        out_specs=(pl.BlockSpec(memory_space=pltpu.VMEM), pl.BlockSpec(memory_space=pltpu.VMEM)),
        scratch_shapes=[
            vmem((users, items), BF16),
            vmem((MASK_SLOTS, users, MASK_COLS), jnp.int32),
            vmem((2, items, dim), BF16),
            vmem((own_i, dim), F32),
            vmem((2, own_i, dim), F32),
            vmem((own_i, dim), F32),
            vmem((2, 2 * CHUNK, dim), F32),
            vmem((2, 2 * CHUNK, dim), F32),
            vmem((3, users, dim), BF16),
            vmem((users, dim), F32),
            vmem((3, own_u, dim), F32),
            vmem((users, 128), F32),
            vmem((users, 128), F32),
            vmem((1, items), F32),
            vmem((1, items), F32),
            vmem((1, items), F32),
            vmem((1, items), F32),
            vmem((8, users), F32),
            vmem((8, users), F32),
            dma((MASK_SLOTS,)),
            dma((3,)), dma((3,)),
            dma((3,)), dma((3,)),
            dma((3,)), dma((3,)),
            dma((3,)), dma((3,)),
            dma((2,)), dma((2,)),
            dma((n_chunk,)), dma((2, n_chunk)),
            dma((n_chunk,)), dma((2, n_chunk)),
            dma((n_chunk,)), dma((2, n_chunk)),
            dma((n_chunk,)), dma((2, n_chunk)),
        ],
        compiler_params=pltpu.CompilerParams(collective_id=0, has_side_effects=True,
                                             vmem_limit_bytes=67_043_328),
    )(mask_blk, user_sh, item_sh)


def lookup_rows(table, ids, offset):
    own_rows = table.shape[0]
    local_ids = ids - offset
    owned = (local_ids >= 0) & (local_ids < own_rows)
    picked = jnp.take(table, jnp.clip(local_ids, 0, own_rows - 1), axis=0)
    return jnp.where(owned[:, None], picked, jnp.zeros((), table.dtype))


def bpr_terms(final_user, final_item, triples, user_off, item_off):
    fetched = jnp.stack([
        lookup_rows(final_user, triples[:, 0], user_off),
        lookup_rows(final_item, triples[:, 1], item_off),
        lookup_rows(final_item, triples[:, 2], item_off)], axis=0)
    mine = lax.psum_scatter(fetched, ("row", "col"), scatter_dimension=1, tiled=True).astype(F32)
    score = lax.psum(jnp.sum(mine[0] * (mine[1] - mine[2]), axis=1), "emb")
    return lax.all_gather(jax.nn.softplus(-score), ("row", "col"), axis=0, tiled=True)


def solution(mesh):
    n_col = mesh.shape["col"]
    n_row = mesh.shape["row"]

    def local_fn(mask_blk, user_sh, item_sh, triples):
        final_user, final_item = propagate(mask_blk, user_sh, item_sh)
        user_off = (lax.axis_index("row") * n_col + lax.axis_index("col")) * final_user.shape[0]
        item_off = (lax.axis_index("col") * n_row + lax.axis_index("row")) * final_item.shape[0]
        return final_user, final_item, bpr_terms(final_user, final_item, triples, user_off, item_off)

    return jax.shard_map(
        local_fn, mesh=mesh,
        in_specs=(P("row", "col"), P(("row", "col"), "emb"), P(("col", "row"), "emb"), P()),
        out_specs=(P(("row", "col"), "emb"), P(("col", "row"), "emb"), P()),
        check_vma=False)
```

time: 601 us -> 362 us (0.60)
  waiting for transfers between devices: 327 us -> 40.5 us
  Pallas kernels: 0 us -> 226 us
  matrix products: 102 us -> 0 us
  other arithmetic: 85.4 us -> 16.3 us
  blocking collectives: 31.6 us -> 20.5 us
    pallas_call x0 -> x1, Pallas kernels: none -> 226 us  [propagate(): pl.pallas_call(prop_kernel, name='propagate', out_shape=(jax.ShapeDtypeSt...]
    reduce_scatter x6 -> x1, waiting for transfers between devices: 179 us -> 40.4 us  [bpr_terms(): lax.psum_scatter(fetched, ('row', 'col'), scatter_dimension=1, tiled=True)]
    psum x2 -> x0, waiting for transfers between devices: 115 us -> none  [the longest x1 96.2 us: bpr_terms(): fetched = lax.psum(fetched, ('row', 'col'))]
    dot_general x6 -> x0, matrix products: 102 us -> none  [the longest x3 51.3 us: local_fn(): lax.dot_general(adj_blk, user_panel, (((0,), (0,)), ((), ())), preferred_...]
    convert_element_type x6 -> x1, other arithmetic: 42.6 us -> 1.05 us  [bpr_terms(): lax.psum_scatter(fetched, ('row', 'col'), scatter_dimension=1, tiled=True)]
    all_gather x3 -> x0, waiting for transfers between devices: 32.1 us -> none  [local_fn(): item_panel = lax.all_gather(item_cur, 'row', axis=0, tiled=True)]
    reduce_sum x2 -> x1, other arithmetic: 24.9 us -> 0.15 us  [bpr_terms(): score = lax.psum(jnp.sum(mine[0] * (mine[1] - mine[2]), axis=1), 'emb')]
    psum x2 -> x1, blocking collectives: 13.7 us -> 4.93 us  [bpr_terms(): score = lax.psum(jnp.sum(mine[0] * (mine[1] - mine[2]), axis=1), 'emb')]
  transfers between devices with their start and end apart: 11 -> 1, of which waited for: 9 -> 1; matrix products, arithmetic and copies ran while one was open for 24% -> 0% of each run, Pallas kernels for 0% -> 0%
where the time goes in v1:
time: 362 us; the launch traced here: 361 us
  Pallas kernels  226 us (62%)
  local copies, waits for them, and re-layouts  44 us (12%)
  waiting for transfers between devices  40.5 us (11%)
  blocking collectives  20.5 us (6%)
  other arithmetic  16.3 us (5%)
  between operations  14.2 us (4%)
    pallas_call x1, Pallas kernels, propagate(): pl.pallas_call(prop_kernel, name='propagate', out_shape=(jax.ShapeDtypeSt...  226 us
    gather x3, local copies, waits for them, and re-layouts, lookup_rows(): picked = jnp.take(table, jnp.clip(local_ids, 0, own_rows - 1), axis=0)  41.7 us
    reduce_scatter x1, waiting for transfers between devices, bpr_terms(): lax.psum_scatter(fetched, ('row', 'col'), scatter_dimension=1, tiled=True)  40.4 us
    all_gather x1, blocking collectives, bpr_terms(): lax.all_gather(jax.nn.softplus(-score), ('row', 'col'), axis=0, tiled=True)  15.5 us
    another operation x2, other arithmetic, bpr_terms(): jnp.stack([lookup_rows(final_user, triples[:, 0], user_off), lookup_rows(...  7.87 us
  transfers between devices with their start and end apart: 1, of which 1 were waited for; matrix products, arithmetic and copies ran while one was open for 0% of the time, Pallas kernels for 0%

profile of v1, /device:TPU:0, one launch (start us, length us, event | category | flops | bytes accessed | tf_op | source)
XLA Modules:
  0.0 361.1 jit_solution(14743960445406721463)
XLA Ops:
  7.2 0.0 reduce-scatter.2.cloned.1.call-start
  7.2 1.0 broadcast_clamp_fusion.2
  8.2 0.6 compare_and_fusion
  8.8 0.6 fusion.6
  9.4 0.6 compare_and_fusion.1
  10.0 0.6 fusion.5
  10.6 1.8 and_reduce_fusion.2
  12.4 0.6 broadcast_clamp_fusion
  13.0 225.7 %propagate.1 = (bf16[512,128]{1,0:T(8,128)(2,1)}, bf16[4096,128]{1,0:T(8,128)(2,1)}) custom-call(s32[1024,16384]{1,0:T(8,128)} %mask_hbm.1, bf16[512,128]{1,0:T(8,128)(2,1)} %eu_ref.1, bf16[4096,128]{1,0:T(8,128)(2,1)} %ei_ref.1), custom_call_target="tpu_custom_call" | custom-call | tf_op jit(solution)/shard_map/propagate/pallas_call | solution.py:281
  238.7 0.0 copy-start.1
  238.7 0.0 copy-start.2
  238.7 14.4 %gather_fusion.2 = bf16[4096,128]{1,0:T(8,128)(2,1)S(1)} fusion(bf16[4096,128]{1,0:T(8,128)(2,1)} %get-tuple-element.24, s32[4096]{0:T(1024)} %fusion.6), kind=kCustom, calls=%fused_computation.1.clone | custom fusion | bytes 2113536 | tf_op jit(solution)/shard_map/jit(_take)/gather | solution.py:328
  253.2 0.0 copy-done.1
  253.2 0.0 copy-done.2
  253.2 0.0 copy-start
  253.2 0.0 copy-start.3
  253.2 15.1 %gather_fusion.1 = bf16[4096,128]{1,0:T(8,128)(2,1)} fusion(bf16[4096,128]{1,0:T(8,128)(2,1)S(1)} %copy-done.1, s32[4096]{0:T(1024)S(1)} %copy-done.2), kind=kCustom, calls=%fused_computation.clone | custom fusion | bytes 2113536 | tf_op jit(solution)/shard_map/jit(_take)/gather | solution.py:328
  268.3 0.0 copy-done
  268.3 0.0 copy-done.3
  268.4 12.1 %gather_fusion = bf16[4096,128]{1,0:T(8,128)(2,1)S(1)} fusion(bf16[512,128]{1,0:T(8,128)(2,1)S(1)} %copy-done, s32[4096]{0:T(1024)S(1)} %copy-done.3), kind=kCustom, calls=%fused_computation.2 | custom fusion | bytes 2113536 | tf_op jit(solution)/shard_map/jit(_take)/gather | solution.py:328
  280.6 1.4 fusion
  282.0 5.9 %fusion.1 = (bf16[1,4096,128]{2,1,0:T(8,128)(2,1)S(1)}, bf16[1,4096,128]{2,1,0:T(8,128)(2,1)S(1)}) fusion(bf16[4096,128]{1,0:T(8,128)(2,1)S(1)} %gather_fusion.2, pred[4096]{0:T(1024)(128)(4,1)S(1)} %copy-done.6, pred[4096]{0:T(1024)(128)(4,1)S(1)} %copy-done.9, bf16[4096,128]{1,0:T(8,128)(2,1)} %gather_fusion.1, pred[4096]{0:T(1024)(128)(4,1)S(1)} %copy-done.7, ...), kind=kLoop, calls=%fused_computation.7 | loop fusion | flops 2097152 | bytes 4210688 | tf_op jit(solution)/shard_map/stack | solution.py:333
  287.9 2.0 pad_maximum_fusion
  289.9 0.0 reduce-scatter.2.cloned.1.call-update
  289.9 40.4 %reduce-scatter.2.cloned.1.call-done = bf16[3,512,128]{2,1,0:T(8,128)(2,1)} async-done(((bf16[3,4096,128]{2,1,0:T(8,128)(2,1)}), bf16[3,512,128]{2,1,0:T(8,128)(2,1)}) %reduce-scatter.2.cloned.1.call-update) | async-done | bytes 393232 | tf_op jit(solution)/shard_map/reduce_scatter | solution.py:337
  330.4 1.0 convert_element_type.3
  331.4 0.1 fusion.4
  331.6 4.9 %psum.7 = f32[512]{0:T(512)S(1)} all-reduce(f32[512]{0:T(512)S(1)} %fusion.4), channel_id=1, replica_groups=mesh['emb'=2,'col'=2,'row'=4] {'emb'}, use_global_device_ids=true, to_apply=%region_2.4 | all-reduce | flops 512 | bytes 4096 | tf_op jit(solution)/shard_map/psum | solution.py:338
  336.5 15.5 %all-gather = f32[8,1,512]{2,1,0:T(1,128)S(1)} all-gather(f32[1,1,512]{2,1,0:T(1,128)S(1)} %bitcast.19), channel_id=1, replica_groups=mesh['emb'=2,'col'=2,'row'=4] {'row','col'}, dimensions={0}, use_global_device_ids=true | all-gather | bytes 18432 | tf_op jit(solution)/shard_map/all_gather | solution.py:339
  352.1 0.7 copy.10
  352.7 1.0 copy.11
  353.7 0.6 copy.12
  (13 shorter events, 0.0 us)
Async XLA Ops:
  7.2 323.2 %reduce-scatter.2.cloned.1.call-start = ((), (), s32[]{:S(2)}) async-start(), calls=%async_computation.1 | async-start | bytes 3538944 | tf_op jit(solution)/shard_map/reduce_scatter | solution.py:337
  238.7 14.5 %copy-start.1 = (bf16[4096,128]{1,0:T(8,128)(2,1)S(1)}, bf16[4096,128]{1,0:T(8,128)(2,1)}, u32[]{:S(2)}) copy-start(bf16[4096,128]{1,0:T(8,128)(2,1)} %get-tuple-element.24) | copy-start | bytes 3145732
  238.7 14.5 %copy-start.2 = (s32[4096]{0:T(1024)S(1)}, s32[4096]{0:T(1024)}, u32[]{:S(2)}) copy-start(s32[4096]{0:T(1024)} %fusion.5) | copy-start | bytes 49156
  253.2 15.1 %copy-start = (bf16[512,128]{1,0:T(8,128)(2,1)S(1)}, bf16[512,128]{1,0:T(8,128)(2,1)}, u32[]{:S(2)}) copy-start(bf16[512,128]{1,0:T(8,128)(2,1)} %get-tuple-element.23) | copy-start | bytes 393220
  253.2 15.1 %copy-start.3 = (s32[4096]{0:T(1024)S(1)}, s32[4096]{0:T(1024)}, u32[]{:S(2)}) copy-start(s32[4096]{0:T(1024)} %broadcast_clamp_fusion) | copy-start | bytes 49156
  268.3 12.2 %copy-start.4 = (pred[4096]{0:T(1024)(128)(4,1)S(1)}, pred[4096]{0:T(1024)(128)(4,1)}, u32[]{:S(2)}) copy-start(pred[4096]{0:T(1024)(128)(4,1)} %get-tuple-element.11) | copy-start | bytes 12292
  268.3 12.2 %copy-start.5 = (pred[4096]{0:T(1024)(128)(4,1)S(1)}, pred[4096]{0:T(1024)(128)(4,1)}, u32[]{:S(2)}) copy-start(pred[4096]{0:T(1024)(128)(4,1)} %get-tuple-element.15) | copy-start | bytes 12292
  268.3 13.6 %copy-start.6 = (pred[4096]{0:T(1024)(128)(4,1)S(1)}, pred[4096]{0:T(1024)(128)(4,1)}, u32[]{:S(2)}) copy-start(pred[4096]{0:T(1024)(128)(4,1)} %compare_and_fusion) | copy-start | bytes 12292
  268.4 13.6 %copy-start.7 = (pred[4096]{0:T(1024)(128)(4,1)S(1)}, pred[4096]{0:T(1024)(128)(4,1)}, u32[]{:S(2)}) copy-start(pred[4096]{0:T(1024)(128)(4,1)} %compare_and_fusion.1) | copy-start | bytes 12292
  268.4 13.6 %copy-start.8 = (pred[4096]{0:T(1024)(128)(4,1)S(1)}, pred[4096]{0:T(1024)(128)(4,1)}, u32[]{:S(2)}) copy-start(pred[4096]{0:T(1024)(128)(4,1)} %get-tuple-element.13) | copy-start | bytes 12292
  268.4 13.6 %copy-start.9 = (pred[4096]{0:T(1024)(128)(4,1)S(1)}, pred[4096]{0:T(1024)(128)(4,1)}, u32[]{:S(2)}) copy-start(pred[4096]{0:T(1024)(128)(4,1)} %get-tuple-element.14) | copy-start | bytes 12292
Sparse Core Ops, SparseCore 0:
  290.0 40.2 reduce-scatter.1

commit v2 on v1

--- a/solution.py
+++ b/solution.py
@@ -13,17 +13,18 @@
 MESH = pl.DeviceIdType.MESH
 
 CHUNK = 512
-MASK_COLS = 512
-MASK_SLOTS = 3
+MASK_COLS = 256
+MASK_SLOTS = 4
 SCALE_ROWS = 256
 FOLD = 1024
 
 
-def prop_kernel(mask_hbm, eu_ref, ei_ref, outu_ref, outi_ref,
-                adj, mbuf, panel, xsend, xrecv, near, stage, drecv, upanel, upart, yrecv,
-                rsum, rscale, csum, ccore, cchip, cfar, rdeg, rdfar,
+def prop_kernel(mask_hbm, eu_ref, ei_ref, trip_ref, outu_ref, outi_ref, loss_ref,
+                adj, mbuf, panel, table, stage, drecv, upanel, upart, yflat,
+                rsum, rscale, csum, ccore, cchip, cfar, rdeg, rdfar, pick_idx, pick_out, pick_in, dots,
                 msem, ag0_s, ag0_r, deg_s, deg_r, u_s, u_r, y_s, y_r,
-                d_s, d_r, x_s, x_r, agx_s, agx_r, agd_s, agd_r, agf_s, agf_r):
+                d_s, d_r, x_s, x_r, agx_s, agx_r, agd_s, agd_r, agf_s, agf_r,
+                fin_s, fin_r, fu_s, fu_r, pick_s, pick_r, dot_s, dot_r, loss_s, loss_r):
     users, items = adj.shape
     own_u = eu_ref.shape[0]
     own_i = ei_ref.shape[0]
@@ -37,6 +38,10 @@
     to_mate = {"row": mate}
     to_far = {"row": far}
     to_col = {"col": other_col}
+    emb = lax.axis_index("emb")
+    to_emb = {"emb": 1 - emb}
+    peers = [{"row": (row + dr) % 4, "col": (col + dc) % 2} for dr in range(4) for dc in range(2)][1:]
+    share = loss_ref.shape[1] // 8
 
     def remote(src, dst, ssem, rsem, target):
         return pltpu.make_async_remote_copy(src_ref=src, dst_ref=dst, send_sem=ssem, recv_sem=rsem,
@@ -46,9 +51,9 @@
         return pl.ds(pl.multiple_of(owner * own_i + j * size, size), size)
 
     barrier = pltpu.get_barrier_semaphore()
-    for target in (to_mate, to_far, to_col):
+    for target in [*peers, to_emb]:
         pl.semaphore_signal(barrier, inc=1, device_id=target, device_id_type=MESH)
-    pl.semaphore_wait(barrier, 3)
+    pl.semaphore_wait(barrier, 8)
 
     block = pl.ds(pl.multiple_of(row * own_i, own_i), own_i)
     far_block = pl.ds(pl.multiple_of(far * own_i, own_i), own_i)
@@ -141,14 +146,30 @@
                                preferred_element_type=F32)
 
     def core_copy(slot):
-        return remote(stage.at[slot], drecv.at[slot], d_s.at[slot], d_r.at[slot], to_mate)
+        return remote(stage.at[slot_rows(slot)], drecv.at[slot_rows(slot)], d_s.at[slot], d_r.at[slot], to_mate)
+
+    def region(k, j):
+        return pl.ds(pl.multiple_of(k * own_i + j * CHUNK, CHUNK), CHUNK)
+
+    def near(j):
+        return region(0, j)
+
+    def arrived(j, layer):
+        return region(1 + layer % 2, j)
+
+    def xsend(j):
+        return region(3, j)
 
     def chunk_rows(j):
         return pl.ds(pl.multiple_of(j * CHUNK, CHUNK), CHUNK)
 
+    def slot_rows(slot, half=None):
+        if half is None:
+            return pl.ds(pl.multiple_of(slot * 2 * CHUNK, 2 * CHUNK), 2 * CHUNK)
+        return pl.ds(pl.multiple_of(slot * 2 * CHUNK + half * CHUNK, CHUNK), CHUNK)
+
     def x_copy(j, layer):
-        par = layer % 2
-        return remote(xsend.at[chunk_rows(j)], xrecv.at[par, chunk_rows(j)], x_s.at[j], x_r.at[par, j], to_far)
+        return remote(table.at[xsend(j)], table.at[arrived(j, layer)], x_s.at[j], x_r.at[layer % 2, j], to_far)
 
     def item_send_step(j, layer):
         slot = j % 2
@@ -160,19 +181,19 @@
             scale_block(mate, j)
         else:
             core_copy(slot).wait_send()
-        stage[slot, 0:CHUNK, :] = item_part(far_mate, j, layer)
-        stage[slot, CHUNK:2 * CHUNK, :] = item_part(mate, j, layer)
+        stage[slot_rows(slot, 0), :] = item_part(far_mate, j, layer)
+        stage[slot_rows(slot, 1), :] = item_part(mate, j, layer)
         core_copy(slot).start()
         if layer == 1:
             scale_block(far, j)
             scale_block(row, j)
         else:
             x_copy(j, layer - 1).wait_send()
-        xsend[chunk_rows(j), :] = item_part(far, j, layer)
-        near[chunk_rows(j), :] = item_part(row, j, layer)
+        table[xsend(j), :] = item_part(far, j, layer)
+        table[near(j), :] = item_part(row, j, layer)
         core_copy(slot).wait_recv()
-        xsend[chunk_rows(j), :] += drecv[slot, 0:CHUNK, :]
-        near[chunk_rows(j), :] += drecv[slot, CHUNK:2 * CHUNK, :]
+        table[xsend(j), :] += drecv[slot_rows(slot, 0), :]
+        table[near(j), :] += drecv[slot_rows(slot, 1), :]
         x_copy(j, layer).start()
 
     def ag_copy(kind, j, layer):
@@ -182,10 +203,29 @@
                               "fwd": (agf_s, agf_r, to_mate)}[kind]
         return remote(block, block, ssem.at[j], rsem.at[par, j], target)
 
+    def fin_copy(kind, j):
+        src, dst, k, target = {
+            "col": (outi_ref.at[chunk_rows(j)], panel.at[1, rows_of(far, j)], 0, to_col),
+            "mate": (outi_ref.at[chunk_rows(j)], panel.at[1, rows_of(row, j)], 1, to_mate),
+            "fwd": (panel.at[1, rows_of(far, j)], panel.at[1, rows_of(far, j)], 2, to_mate)}[kind]
+        return remote(src, dst, fin_s.at[k, j], fin_r.at[k, j], target)
+
+    def fin_near(j):
+        fin_copy("col", j).wait_recv()
+        fin_copy("fwd", j).start()
+        table[region(2, j), :] = panel[1, rows_of(far, j), :].astype(F32)
+        fin_copy("mate", j).wait_recv()
+        table[region(1, j), :] = panel[1, rows_of(mate, j), :].astype(F32)
+
+    def fin_fwd(j):
+        x_copy(j, NUM_LAYERS).wait_send()
+        fin_copy("fwd", j).wait_recv()
+        table[region(3, j), :] = panel[1, rows_of(far_mate, j), :].astype(F32)
+
     def finish_item(j, layer):
         x_copy(j, layer).wait_recv()
         par = layer % 2
-        value = (near[chunk_rows(j), :] + xrecv[par, chunk_rows(j), :]).astype(BF16)
+        value = (table[near(j), :] + table[arrived(j, layer), :]).astype(BF16)
         if layer < NUM_LAYERS:
             panel[par, rows_of(row, j), :] = value
             ag_copy("x", j, layer).start()
@@ -194,7 +234,11 @@
             total = ei_ref[chunk_rows(j), :].astype(F32) + panel[1, rows_of(row, j), :].astype(F32)
             total = total + panel[0, rows_of(row, j), :].astype(F32)
             total = total + value.astype(F32)
-            outi_ref[chunk_rows(j), :] = (total / (NUM_LAYERS + 1)).astype(BF16)
+            final = (total / (NUM_LAYERS + 1)).astype(BF16)
+            outi_ref[chunk_rows(j), :] = final
+            table[near(j), :] = final.astype(F32)
+            fin_copy("col", j).start()
+            fin_copy("mate", j).start()
 
     def gather_items(layer):
         def forward(j, carry):
@@ -223,15 +267,18 @@
 
         lax.fori_loop(0, items // FOLD, fold, 0)
 
+    def yrows(layer):
+        return pl.ds((layer - 1) * own_u, own_u)
+
     def y_copy(layer):
-        return remote(upart.at[oblock], yrecv.at[layer - 1], y_s.at[layer - 1], y_r.at[layer - 1], to_col)
+        return remote(upart.at[oblock], yflat.at[yrows(layer)], y_s.at[layer - 1], y_r.at[layer - 1], to_col)
 
     def u_copy(layer):
         return remote(upanel.at[layer, ublock], upanel.at[layer, ublock], u_s.at[layer], u_r.at[layer], to_col)
 
     def finish_user(layer):
         y_copy(layer).wait()
-        value = (upart[ublock, :] + yrecv[layer - 1]).astype(BF16)
+        value = (upart[ublock, :] + yflat[yrows(layer), :]).astype(BF16)
         if layer < NUM_LAYERS:
             upanel[layer, ublock, :] = value
             u_copy(layer).start()
@@ -239,7 +286,69 @@
             total = eu_ref[...].astype(F32) + upanel[1, ublock, :].astype(F32)
             total = total + upanel[2, ublock, :].astype(F32)
             total = total + value.astype(F32)
-            outu_ref[...] = (total / (NUM_LAYERS + 1)).astype(BF16)
+            final = (total / (NUM_LAYERS + 1)).astype(BF16)
+            outu_ref[...] = final
+            stage[0:own_u, :] = final.astype(F32)
+            fu_copy("col").start()
+            fu_copy("mate").start()
+
+    def fu_copy(kind):
+        src, dst, k, target = {
+            "col": (outu_ref, upanel.at[0, pl.ds(0, own_u)], 0, to_col),
+            "mate": (outu_ref, upanel.at[0, pl.ds(own_u, own_u)], 1, to_mate),
+            "fwd": (upanel.at[0, pl.ds(0, own_u)], upanel.at[1, oblock], 2, to_mate)}[kind]
+        return remote(src, dst, fu_s.at[k], fu_r.at[k], target)
+
+    def gather_users():
+        fu_copy("col").wait_recv()
+        fu_copy("fwd").start()
+        stage[2 * own_u:3 * own_u, :] = upanel[0, 0:own_u, :].astype(F32)
+        fu_copy("mate").wait_recv()
+        stage[own_u:2 * own_u, :] = upanel[0, own_u:2 * own_u, :].astype(F32)
+        fu_copy("fwd").wait_recv()
+        stage[3 * own_u:4 * own_u, :] = upanel[1, oblock, :].astype(F32)
+
+    def place_rows():
+        def side(r):
+            return r // 2
+
+        def step(t, carry):
+            for k, owner in ((0, far), (1, row)):
+                base = (owner * 2 + col) * share + t
+                user = trip_ref[0, base]
+                ur = lax.shift_right_logical(user, 10)
+                uc = lax.bitwise_and(lax.shift_right_logical(user, 9), 1)
+                pos = (jnp.where(uc == col, 0, 2) + jnp.where(ur == row, 0, 1)) * own_u + lax.bitwise_and(user, 511)
+                pick_idx[k * 3 * share + t] = jnp.where(lax.shift_right_logical(ur, 1) == side(row), pos, 4 * own_u)
+                for which in (1, 2):
+                    item = trip_ref[which, base]
+                    ic = lax.shift_right_logical(item, 14)
+                    ir = lax.bitwise_and(lax.shift_right_logical(item, 12), 3)
+                    pos = (jnp.where(ic == col, 0, 2) + jnp.where(ir == row, 0, 1)) * own_i + lax.bitwise_and(item, 4095)
+                    pick_idx[(k * 3 + which) * share + t] = jnp.where(
+                        lax.shift_right_logical(ir, 1) == side(row), pos, 4 * own_i)
+            return carry
+
+        lax.fori_loop(0, share, step, 0)
+
+    def pick(src, k, which, dst):
+        def step(t, carry):
+            for i in range(8):
+                at = t * 8 + i
+                dst[pl.ds(which * share + at, 1), :] = src[pl.ds(pick_idx[(k * 3 + which) * share + at], 1), :]
+            return carry
+
+        lax.fori_loop(0, share // 8, step, 0)
+
+    def pick_copy(which):
+        rows = pl.ds(which * share, share)
+        return remote(pick_out.at[rows], pick_in.at[rows], pick_s.at[which], pick_r.at[which], to_far)
+
+    def pick_far(src, which):
+        pick(src, 0, which, yflat)
+        rows = pl.ds(which * share, share)
+        pick_out[rows, :] = yflat[rows, :].astype(BF16)
+        pick_copy(which).start()
 
     def loop(lo, hi, body):
         def step(j, carry):
@@ -260,43 +369,97 @@
             gather_items(layer - 1)
         user_part(layer)
         y_copy(layer).start()
-        loop(0, n_chunk // 2, functools.partial(finish_item, layer=layer))
-        finish_user(layer)
-        loop(n_chunk // 2, n_chunk, functools.partial(finish_item, layer=layer))
         if layer < NUM_LAYERS:
+            loop(0, n_chunk // 2, functools.partial(finish_item, layer=layer))
+            finish_user(layer)
+            loop(n_chunk // 2, n_chunk, functools.partial(finish_item, layer=layer))
             u_copy(layer).wait()
 
     for slot in range(2):
         core_copy(slot).wait_send()
-    for j in range(n_chunk):
-        x_copy(j, NUM_LAYERS).wait_send()
-
-
-def propagate(mask_blk, user_sh, item_sh):
+    table[pl.ds(4 * own_i, 8), :] = jnp.zeros((8, 128), F32)
+    stage[pl.ds(4 * own_u, 8), :] = jnp.zeros((8, 128), F32)
+    place_rows()
+    finish_user(NUM_LAYERS)
+
+    def last_step(j):
+        finish_item(j, NUM_LAYERS)
+
+        @pl.when(j >= 1)
+        def _():
+            fin_near(j - 1)
+
+        @pl.when(j >= 2)
+        def _():
+            fin_fwd(j - 2)
+
+    loop(0, n_chunk // 2, last_step)
+    gather_users()
+    pick_far(stage, 0)
+    pick(stage, 1, 0, drecv)
+    loop(n_chunk // 2, n_chunk, last_step)
+    fin_near(n_chunk - 1)
+    fin_fwd(n_chunk - 2)
+    fin_fwd(n_chunk - 1)
+    pick_far(table, 1)
+    pick_far(table, 2)
+    pick(table, 1, 1, drecv)
+    pick(table, 1, 2, drecv)
+
+    def both(which):
+        rows = pl.ds(which * share, share)
+        pick_copy(which).wait_recv()
+        return drecv[rows, :] + pick_in[rows, :].astype(F32)
+
+    e_user, e_pos, e_neg = both(0), both(1), both(2)
+    prod = e_user * (e_pos - e_neg)
+    dots[0] = jnp.sum(prod.T, axis=0, keepdims=True)
+    dot_copy = remote(dots.at[0], dots.at[1], dot_s.at[0], dot_r.at[0], to_emb)
+    dot_copy.start()
+    dot_copy.wait()
+    z = -(dots[0] + dots[1])
+    mine = pl.ds(pl.multiple_of((row * 2 + col) * share, share), share)
+    loss_ref[:, mine] = jnp.maximum(z, 0.0) + jnp.log1p(jnp.exp(-jnp.abs(z)))
+    copies = [remote(loss_ref.at[:, mine], loss_ref.at[:, mine], loss_s.at[k], loss_r.at[k], target)
+              for k, target in enumerate(peers)]
+    for copy in copies:
+        copy.start()
+
+    for which in range(3):
+        pick_copy(which).wait_send()
+    for kind in ("col", "mate", "fwd"):
+        fu_copy(kind).wait_send()
+        loop(0, n_chunk, lambda j: fin_copy(kind, j).wait_send())
+    for copy in copies:
+        copy.wait()
+
+
+def propagate(mask_blk, user_sh, item_sh, triples):
     users, items = mask_blk.shape
     own_u, dim = user_sh.shape
     own_i = item_sh.shape[0]
     n_chunk = own_i // CHUNK
+    num_trip = triples.shape[0]
+    share = num_trip // 8
     vmem, dma = pltpu.VMEM, pltpu.SemaphoreType.DMA
     return pl.pallas_call(
         prop_kernel,
         name="propagate",
-        out_shape=(jax.ShapeDtypeStruct((own_u, dim), BF16), jax.ShapeDtypeStruct((own_i, dim), BF16)),
+        out_shape=(jax.ShapeDtypeStruct((own_u, dim), BF16), jax.ShapeDtypeStruct((own_i, dim), BF16),
+                   jax.ShapeDtypeStruct((1, num_trip), F32)),
         in_specs=[pl.BlockSpec(memory_space=pl.ANY), pl.BlockSpec(memory_space=pltpu.VMEM),
-                  pl.BlockSpec(memory_space=pltpu.VMEM)],
-        out_specs=(pl.BlockSpec(memory_space=pltpu.VMEM), pl.BlockSpec(memory_space=pltpu.VMEM)),
+                  pl.BlockSpec(memory_space=pltpu.VMEM), pl.BlockSpec(memory_space=pltpu.SMEM)],
+        out_specs=(pl.BlockSpec(memory_space=pltpu.VMEM),) * 3,
         scratch_shapes=[
             vmem((users, items), BF16),
             vmem((MASK_SLOTS, users, MASK_COLS), jnp.int32),
             vmem((2, items, dim), BF16),
-            vmem((own_i, dim), F32),
-            vmem((2, own_i, dim), F32),
-            vmem((own_i, dim), F32),
-            vmem((2, 2 * CHUNK, dim), F32),
-            vmem((2, 2 * CHUNK, dim), F32),
+            vmem((4 * own_i + 8, dim), F32),
+            vmem((4 * CHUNK + 8, dim), F32),
+            vmem((4 * CHUNK, dim), F32),
             vmem((3, users, dim), BF16),
             vmem((users, dim), F32),
-            vmem((3, own_u, dim), F32),
+            vmem((3 * own_u, dim), F32),
             vmem((users, 128), F32),
             vmem((users, 128), F32),
             vmem((1, items), F32),
@@ -305,6 +468,10 @@
             vmem((1, items), F32),
             vmem((8, users), F32),
             vmem((8, users), F32),
+            pltpu.SMEM((6 * share,), jnp.int32),
+            vmem((3 * share, dim), BF16),
+            vmem((3 * share, dim), BF16),
+            vmem((2, 1, share), F32),
             dma((MASK_SLOTS,)),
             dma((3,)), dma((3,)),
             dma((3,)), dma((3,)),
@@ -315,39 +482,21 @@
             dma((n_chunk,)), dma((2, n_chunk)),
             dma((n_chunk,)), dma((2, n_chunk)),
             dma((n_chunk,)), dma((2, n_chunk)),
+            dma((3, n_chunk)), dma((3, n_chunk)),
+            dma((3,)), dma((3,)),
+            dma((3,)), dma((3,)),
+            dma((1,)), dma((1,)),
+            dma((7,)), dma((7,)),
         ],
         compiler_params=pltpu.CompilerParams(collective_id=0, has_side_effects=True,
                                              vmem_limit_bytes=67_043_328),
-    )(mask_blk, user_sh, item_sh)
-
-
-def lookup_rows(table, ids, offset):
-    own_rows = table.shape[0]
-    local_ids = ids - offset
-    owned = (local_ids >= 0) & (local_ids < own_rows)
-    picked = jnp.take(table, jnp.clip(local_ids, 0, own_rows - 1), axis=0)
-    return jnp.where(owned[:, None], picked, jnp.zeros((), table.dtype))
-
-
-def bpr_terms(final_user, final_item, triples, user_off, item_off):
-    fetched = jnp.stack([
-        lookup_rows(final_user, triples[:, 0], user_off),
-        lookup_rows(final_item, triples[:, 1], item_off),
-        lookup_rows(final_item, triples[:, 2], item_off)], axis=0)
-    mine = lax.psum_scatter(fetched, ("row", "col"), scatter_dimension=1, tiled=True).astype(F32)
-    score = lax.psum(jnp.sum(mine[0] * (mine[1] - mine[2]), axis=1), "emb")
-    return lax.all_gather(jax.nn.softplus(-score), ("row", "col"), axis=0, tiled=True)
+    )(mask_blk, user_sh, item_sh, triples.T)
 
 
 def solution(mesh):
-    n_col = mesh.shape["col"]
-    n_row = mesh.shape["row"]
-
     def local_fn(mask_blk, user_sh, item_sh, triples):
-        final_user, final_item = propagate(mask_blk, user_sh, item_sh)
-        user_off = (lax.axis_index("row") * n_col + lax.axis_index("col")) * final_user.shape[0]
-        item_off = (lax.axis_index("col") * n_row + lax.axis_index("row")) * final_item.shape[0]
-        return final_user, final_item, bpr_terms(final_user, final_item, triples, user_off, item_off)
+        final_user, final_item, loss = propagate(mask_blk, user_sh, item_sh, triples)
+        return final_user, final_item, loss.reshape(-1)
 
     return jax.shard_map(
         local_fn, mesh=mesh,

time: 362 us -> 273 us (0.75)
  Pallas kernels: 226 us -> 267 us
  waiting for transfers between devices: 40.5 us -> 0 us
  local copies, waits for them, and re-layouts: 44 us -> 5.15 us
  blocking collectives: 20.5 us -> 0 us
  other arithmetic: 16.3 us -> 0 us
  between operations: 14.2 us -> 0.64 us
    gather x3 -> x0, local copies, waits for them, and re-layouts: 41.7 us -> none  [lookup_rows(): picked = jnp.take(table, jnp.clip(local_ids, 0, own_rows - 1), axis=0)]
    pallas_call x1, Pallas kernels: 226 us -> 267 us  [propagate(): pl.pallas_call(prop_kernel, name='propagate', out_shape=(jax.ShapeDtypeSt...]
    reduce_scatter x1 -> x0, waiting for transfers between devices: 40.4 us -> none  [bpr_terms(): lax.psum_scatter(fetched, ('row', 'col'), scatter_dimension=1, tiled=True)]
    all_gather x1 -> x0, blocking collectives: 15.5 us -> none  [bpr_terms(): lax.all_gather(jax.nn.softplus(-score), ('row', 'col'), axis=0, tiled=True)]
    another operation x2 -> x0, other arithmetic: 7.87 us -> none  [bpr_terms(): jnp.stack([lookup_rows(final_user, triples[:, 0], user_off), lookup_rows(...]
    psum x1 -> x0, blocking collectives: 4.93 us -> none  [bpr_terms(): score = lax.psum(jnp.sum(mine[0] * (mine[1] - mine[2]), axis=1), 'emb')]
  transfers between devices with their start and end apart: 1 -> 0, of which waited for: 1 -> 0; matrix products, arithmetic and copies ran while one was open for 0% -> 0% of each run, Pallas kernels for 0% -> 0%
where the time goes in v2:
time: 273 us
  Pallas kernels  267 us (98%)
  local copies, waits for them, and re-layouts  5.15 us (2%)
    pallas_call x1, Pallas kernels, propagate(): pl.pallas_call(prop_kernel, name='propagate', out_shape=(jax.ShapeDtypeSt...  267 us

profile of v2, /device:TPU:0, one launch (start us, length us, event | category | flops | bytes accessed | tf_op | source)
XLA Modules:
  0.0 273.0 jit_solution(16773203899392463073)
XLA Ops:
  0.6 267.2 %propagate.1 = (bf16[512,128]{1,0:T(8,128)(2,1)}, bf16[4096,128]{1,0:T(8,128)(2,1)}, f32[1,4096]{1,0:T(1,128)}) custom-call(s32[1024,16384]{1,0:T(8,128)} %mask_hbm.1, bf16[512,128]{1,0:T(8,128)(2,1)} %eu_ref.1, bf16[4096,128]{1,0:T(8,128)(2,1)} %ei_ref.1, s32[3,4096]{1,0:T(4,128)} %bitcast.2), custom_call_target="tpu_custom_call" | custom-call | tf_op jit(solution)/shard_map/propagate/pallas_call | solution.py:445
  267.8 1.6 copy.10
  269.4 2.3 copy.11
  271.7 1.3 copy.12

commit v3 on v2

--- a/solution.py
+++ b/solution.py
@@ -12,20 +12,24 @@
 BF16 = jnp.bfloat16
 MESH = pl.DeviceIdType.MESH
 
-CHUNK = 512
+CHUNK = 256
 MASK_COLS = 256
-MASK_SLOTS = 4
+MASK_SLOTS = 7
+PIECES = 16
+CORE_SLOTS = 4
 SCALE_ROWS = 256
-FOLD = 1024
+LAG = 3
+FOLD = 2048
 
 
 def prop_kernel(mask_hbm, eu_ref, ei_ref, trip_ref, outu_ref, outi_ref, loss_ref,
                 adj, mbuf, panel, table, stage, drecv, upanel, upart, yflat,
-                rsum, rscale, csum, ccore, cchip, cfar, rdeg, rdfar, pick_idx, pick_out, pick_in, dots,
+                csum, ccore, cchip, cfar, rdeg, rdfar, pick_idx, pick_in, dots,
                 msem, ag0_s, ag0_r, deg_s, deg_r, u_s, u_r, y_s, y_r,
                 d_s, d_r, x_s, x_r, agx_s, agx_r, agd_s, agd_r, agf_s, agf_r,
-                fin_s, fin_r, fu_s, fu_r, pick_s, pick_r, dot_s, dot_r, loss_s, loss_r):
+                fin_s, fin_r, fu_s, fu_r, pick_s, pick_r, dot_s, dot_r, out_s, loss_s, loss_r):
     users, items = adj.shape
+    rsum = rscale = upart
     own_u = eu_ref.shape[0]
     own_i = ei_ref.shape[0]
     n_chunk = own_i // CHUNK
@@ -172,9 +176,9 @@
         return remote(table.at[xsend(j)], table.at[arrived(j, layer)], x_s.at[j], x_r.at[layer % 2, j], to_far)
 
     def item_send_step(j, layer):
-        slot = j % 2
+        slot = j % CORE_SLOTS
         if layer == 1:
-            @pl.when(j >= 2)
+            @pl.when(j >= CORE_SLOTS)
             def _():
                 core_copy(slot).wait_send()
             scale_block(far_mate, j)
@@ -191,6 +195,17 @@
             x_copy(j, layer - 1).wait_send()
         table[xsend(j), :] = item_part(far, j, layer)
         table[near(j), :] = item_part(row, j, layer)
+
+        @pl.when(j == 0)
+        def _():
+            add_mate(0, layer)
+
+        @pl.when(j >= 2)
+        def _():
+            add_mate(j - 1, layer)
+
+    def add_mate(j, layer):
+        slot = j % CORE_SLOTS
         core_copy(slot).wait_recv()
         table[xsend(j), :] += drecv[slot_rows(slot, 0), :]
         table[near(j), :] += drecv[slot_rows(slot, 1), :]
@@ -205,10 +220,13 @@
 
     def fin_copy(kind, j):
         src, dst, k, target = {
-            "col": (outi_ref.at[chunk_rows(j)], panel.at[1, rows_of(far, j)], 0, to_col),
-            "mate": (outi_ref.at[chunk_rows(j)], panel.at[1, rows_of(row, j)], 1, to_mate),
+            "col": (panel.at[1, rows_of(row, j)], panel.at[1, rows_of(far, j)], 0, to_col),
+            "mate": (panel.at[1, rows_of(row, j)], panel.at[1, rows_of(row, j)], 1, to_mate),
             "fwd": (panel.at[1, rows_of(far, j)], panel.at[1, rows_of(far, j)], 2, to_mate)}[kind]
         return remote(src, dst, fin_s.at[k, j], fin_r.at[k, j], target)
+
+    def out_copy(j):
+        return pltpu.make_async_copy(panel.at[1, rows_of(row, j)], outi_ref.at[chunk_rows(j)], out_s.at[j])
 
     def fin_near(j):
         fin_copy("col", j).wait_recv()
@@ -235,10 +253,11 @@
             total = total + panel[0, rows_of(row, j), :].astype(F32)
             total = total + value.astype(F32)
             final = (total / (NUM_LAYERS + 1)).astype(BF16)
-            outi_ref[chunk_rows(j), :] = final
+            panel[1, rows_of(row, j), :] = final
             table[near(j), :] = final.astype(F32)
             fin_copy("col", j).start()
             fin_copy("mate", j).start()
+            out_copy(j).start()
 
     def gather_items(layer):
         def forward(j, carry):
@@ -308,7 +327,7 @@
         fu_copy("fwd").wait_recv()
         stage[3 * own_u:4 * own_u, :] = upanel[1, oblock, :].astype(F32)
 
-    def place_rows():
+    def place_rows(piece):
         def side(r):
             return r // 2
 
@@ -329,7 +348,7 @@
                         lax.shift_right_logical(ir, 1) == side(row), pos, 4 * own_i)
             return carry
 
-        lax.fori_loop(0, share, step, 0)
+        lax.fori_loop(piece * (share // PIECES), (piece + 1) * (share // PIECES), step, 0)
 
     def pick(src, k, which, dst):
         def step(t, carry):
@@ -340,14 +359,17 @@
 
         lax.fori_loop(0, share // 8, step, 0)
 
+    def out_rows(which):
+        return pl.ds(pl.multiple_of(far * own_i + which * share, share), share)
+
     def pick_copy(which):
         rows = pl.ds(which * share, share)
-        return remote(pick_out.at[rows], pick_in.at[rows], pick_s.at[which], pick_r.at[which], to_far)
+        return remote(panel.at[0, out_rows(which)], pick_in.at[rows], pick_s.at[which], pick_r.at[which], to_far)
 
     def pick_far(src, which):
         pick(src, 0, which, yflat)
         rows = pl.ds(which * share, share)
-        pick_out[rows, :] = yflat[rows, :].astype(BF16)
+        panel[0, out_rows(which), :] = yflat[rows, :].astype(BF16)
         pick_copy(which).start()
 
     def loop(lo, hi, body):
@@ -358,6 +380,7 @@
 
     for layer in range(1, NUM_LAYERS + 1):
         loop(0, n_chunk, functools.partial(item_send_step, layer=layer))
+        add_mate(n_chunk - 1, layer)
         if layer == 1:
             ag0_d.wait_recv()
             ag0_f.wait_recv()
@@ -371,36 +394,39 @@
         y_copy(layer).start()
         if layer < NUM_LAYERS:
             loop(0, n_chunk // 2, functools.partial(finish_item, layer=layer))
+            if layer == 1:
+                loop(0, 4, place_rows)
             finish_user(layer)
+            if layer > 1:
+                loop(4, PIECES, place_rows)
             loop(n_chunk // 2, n_chunk, functools.partial(finish_item, layer=layer))
             u_copy(layer).wait()
 
-    for slot in range(2):
+    for slot in range(CORE_SLOTS):
         core_copy(slot).wait_send()
     table[pl.ds(4 * own_i, 8), :] = jnp.zeros((8, 128), F32)
     stage[pl.ds(4 * own_u, 8), :] = jnp.zeros((8, 128), F32)
-    place_rows()
-    finish_user(NUM_LAYERS)
 
     def last_step(j):
         finish_item(j, NUM_LAYERS)
 
-        @pl.when(j >= 1)
+        @pl.when(j >= LAG)
         def _():
-            fin_near(j - 1)
-
-        @pl.when(j >= 2)
+            fin_near(j - LAG)
+
+        @pl.when(j >= LAG + 2)
         def _():
-            fin_fwd(j - 2)
+            fin_fwd(j - LAG - 2)
 
     loop(0, n_chunk // 2, last_step)
+    finish_user(NUM_LAYERS)
+    loop(n_chunk // 2, 3 * n_chunk // 4, last_step)
     gather_users()
     pick_far(stage, 0)
     pick(stage, 1, 0, drecv)
-    loop(n_chunk // 2, n_chunk, last_step)
-    fin_near(n_chunk - 1)
-    fin_fwd(n_chunk - 2)
-    fin_fwd(n_chunk - 1)
+    loop(3 * n_chunk // 4, n_chunk, last_step)
+    loop(n_chunk - LAG, n_chunk, fin_near)
+    loop(n_chunk - LAG - 2, n_chunk, fin_fwd)
     pick_far(table, 1)
     pick_far(table, 2)
     pick(table, 1, 1, drecv)
@@ -430,6 +456,7 @@
     for kind in ("col", "mate", "fwd"):
         fu_copy(kind).wait_send()
         loop(0, n_chunk, lambda j: fin_copy(kind, j).wait_send())
+    loop(0, n_chunk, lambda j: out_copy(j).wait())
     for copy in copies:
         copy.wait()
 
@@ -449,19 +476,18 @@
                    jax.ShapeDtypeStruct((1, num_trip), F32)),
         in_specs=[pl.BlockSpec(memory_space=pl.ANY), pl.BlockSpec(memory_space=pltpu.VMEM),
                   pl.BlockSpec(memory_space=pltpu.VMEM), pl.BlockSpec(memory_space=pltpu.SMEM)],
-        out_specs=(pl.BlockSpec(memory_space=pltpu.VMEM),) * 3,
+        out_specs=(pl.BlockSpec(memory_space=pltpu.VMEM), pl.BlockSpec(memory_space=pl.ANY),
+                   pl.BlockSpec(memory_space=pltpu.VMEM)),
         scratch_shapes=[
             vmem((users, items), BF16),
             vmem((MASK_SLOTS, users, MASK_COLS), jnp.int32),
             vmem((2, items, dim), BF16),
             vmem((4 * own_i + 8, dim), F32),
-            vmem((4 * CHUNK + 8, dim), F32),
-            vmem((4 * CHUNK, dim), F32),
+            vmem((CORE_SLOTS * 2 * CHUNK + 8, dim), F32),
+            vmem((CORE_SLOTS * 2 * CHUNK, dim), F32),
             vmem((3, users, dim), BF16),
             vmem((users, dim), F32),
             vmem((3 * own_u, dim), F32),
-            vmem((users, 128), F32),
-            vmem((users, 128), F32),
             vmem((1, items), F32),
             vmem((1, items), F32),
             vmem((1, items), F32),
@@ -470,14 +496,13 @@
             vmem((8, users), F32),
             pltpu.SMEM((6 * share,), jnp.int32),
             vmem((3 * share, dim), BF16),
-            vmem((3 * share, dim), BF16),
             vmem((2, 1, share), F32),
             dma((MASK_SLOTS,)),
             dma((3,)), dma((3,)),
             dma((3,)), dma((3,)),
             dma((3,)), dma((3,)),
             dma((3,)), dma((3,)),
-            dma((2,)), dma((2,)),
+            dma((CORE_SLOTS,)), dma((CORE_SLOTS,)),
             dma((n_chunk,)), dma((2, n_chunk)),
             dma((n_chunk,)), dma((2, n_chunk)),
             dma((n_chunk,)), dma((2, n_chunk)),
@@ -486,6 +511,7 @@
             dma((3,)), dma((3,)),
             dma((3,)), dma((3,)),
             dma((1,)), dma((1,)),
+            dma((n_chunk,)),
             dma((7,)), dma((7,)),
         ],
         compiler_params=pltpu.CompilerParams(collective_id=0, has_side_effects=True,

time: 273 us -> 247 us (0.905)
  Pallas kernels: 267 us -> 241 us
    pallas_call x1, Pallas kernels: 267 us -> 241 us  [propagate(): pl.pallas_call(prop_kernel, name='propagate', out_shape=(jax.ShapeDtypeSt...]
where the time goes in v3:
time: 247 us
  Pallas kernels  241 us (98%)
  local copies, waits for them, and re-layouts  5.15 us (2%)
    pallas_call x1, Pallas kernels, propagate(): pl.pallas_call(prop_kernel, name='propagate', out_shape=(jax.ShapeDtypeSt...  241 us
    unnamed x3, local copies, waits for them, and re-layouts  5.15 us

profile of v3, /device:TPU:0, one launch (start us, length us, event | category | flops | bytes accessed | tf_op | source)
XLA Modules:
  0.0 246.6 jit_solution(17145808039321848140)
XLA Ops:
  0.6 240.8 %propagate.1 = (bf16[512,128]{1,0:T(8,128)(2,1)}, bf16[4096,128]{1,0:T(8,128)(2,1)}, f32[1,4096]{1,0:T(1,128)}) custom-call(s32[1024,16384]{1,0:T(8,128)} %mask_hbm.1, bf16[512,128]{1,0:T(8,128)(2,1)} %eu_ref.1, bf16[4096,128]{1,0:T(8,128)(2,1)} %ei_ref.1, s32[3,4096]{1,0:T(4,128)} %bitcast.2), custom_call_target="tpu_custom_call" | custom-call | tf_op jit(solution)/shard_map/propagate/pallas_call | solution.py:472
  241.4 1.6 copy.10
  243.0 2.3 copy.11
  245.2 1.3 copy.12

commit v4 on v3

--- a/solution.py
+++ b/solution.py
@@ -13,8 +13,8 @@
 MESH = pl.DeviceIdType.MESH
 
 CHUNK = 256
-MASK_COLS = 256
 MASK_SLOTS = 7
+EARLY = 12
 PIECES = 16
 CORE_SLOTS = 4
 SCALE_ROWS = 256
@@ -22,12 +22,12 @@
 FOLD = 2048
 
 
-def prop_kernel(mask_hbm, eu_ref, ei_ref, trip_ref, outu_ref, outi_ref, loss_ref,
-                adj, mbuf, panel, table, stage, drecv, upanel, upart, yflat,
+def prop_kernel(mask_hbm, eu_hbm, ei_hbm, trip_hbm, outu_ref, outi_ref, loss_ref,
+                adj, mbuf, panel, table, stage, drecv, upanel, upart, yflat, eu_ref, ei_ref, trip_ref,
                 csum, ccore, cchip, cfar, rdeg, rdfar, pick_idx, pick_in, dots,
-                msem, ag0_s, ag0_r, deg_s, deg_r, u_s, u_r, y_s, y_r,
+                in_s, msem, ag0_s, ag0_r, deg_s, deg_r, u_s, u_r, y_s, y_r,
                 d_s, d_r, x_s, x_r, agx_s, agx_r, agd_s, agd_r, agf_s, agf_r,
-                fin_s, fin_r, fu_s, fu_r, pick_s, pick_r, dot_s, dot_r, out_s, loss_s, loss_r):
+                fin_s, fin_r, fu_s, fu_r, pick_s, pick_r, out_s, loss_s, loss_r):
     users, items = adj.shape
     rsum = rscale = upart
     own_u = eu_ref.shape[0]
@@ -43,8 +43,8 @@
     to_far = {"row": far}
     to_col = {"col": other_col}
     emb = lax.axis_index("emb")
-    to_emb = {"emb": 1 - emb}
-    peers = [{"row": (row + dr) % 4, "col": (col + dc) % 2} for dr in range(4) for dc in range(2)][1:]
+    peers = [{"emb": (emb + de) % 2, "row": (row + dr) % 4, "col": (col + dc) % 2}
+             for de in range(2) for dr in range(4) for dc in range(2)][1:]
     share = loss_ref.shape[1] // 8
 
     def remote(src, dst, ssem, rsem, target):
@@ -53,35 +53,45 @@
 
     def rows_of(owner, j, size=CHUNK):
         return pl.ds(pl.multiple_of(owner * own_i + j * size, size), size)
-
-    barrier = pltpu.get_barrier_semaphore()
-    for target in [*peers, to_emb]:
-        pl.semaphore_signal(barrier, inc=1, device_id=target, device_id_type=MESH)
-    pl.semaphore_wait(barrier, 8)
 
     block = pl.ds(pl.multiple_of(row * own_i, own_i), own_i)
     far_block = pl.ds(pl.multiple_of(far * own_i, own_i), own_i)
     ublock = pl.ds(pl.multiple_of(col * own_u, own_u), own_u)
     oblock = pl.ds(pl.multiple_of(other_col * own_u, own_u), own_u)
-    ag0_x = remote(ei_ref, panel.at[0, block], ag0_s.at[0], ag0_r.at[0], to_far)
-    ag0_d = remote(ei_ref, panel.at[0, block], ag0_s.at[1], ag0_r.at[1], to_mate)
-    ag0_f = remote(panel.at[0, far_block], panel.at[0, far_block], ag0_s.at[2], ag0_r.at[2], to_mate)
-    ag0_x.start()
-    ag0_d.start()
-    u0 = remote(eu_ref, upanel.at[0, ublock], u_s.at[0], u_r.at[0], to_col)
-    u0.start()
-
-    n_mask = items // MASK_COLS
+    n_mask = items // CHUNK
 
     def mask_copy(i):
-        cols = pl.ds(pl.multiple_of(i * MASK_COLS, MASK_COLS), MASK_COLS)
         slot = i % MASK_SLOTS
-        return pltpu.make_async_copy(mask_hbm.at[:, cols], mbuf.at[slot], msem.at[slot])
+        return pltpu.make_async_copy(mask_hbm.at[:, rows_of(i % 4, i // 4)], mbuf.at[slot], msem.at[slot])
 
     for i in range(MASK_SLOTS - 1):
         mask_copy(i).start()
-    panel[0, block, :] = ei_ref[...]
-    upanel[0, ublock, :] = eu_ref[...]
+    inputs = [pltpu.make_async_copy(src, dst, in_s.at[k]) for k, (src, dst) in enumerate((
+        (eu_hbm, upanel.at[0, ublock]), (ei_hbm, panel.at[0, block]), (eu_hbm, eu_ref), (ei_hbm, ei_ref),
+        (trip_hbm, trip_ref)))]
+    for copy in inputs:
+        copy.start()
+
+    barrier = pltpu.get_barrier_semaphore()
+    for target in peers:
+        pl.semaphore_signal(barrier, inc=1, device_id=target, device_id_type=MESH)
+    pl.semaphore_wait(barrier, len(peers))
+
+    quarter = own_i // 4
+
+    def ag0_x(k):
+        return remote(ei_hbm.at[pl.ds(k * quarter, quarter)],
+                      panel.at[0, pl.ds(pl.multiple_of(row * own_i + k * quarter, quarter), quarter)],
+                      ag0_s.at[k], ag0_r.at[k], to_far)
+
+    ag0_d = remote(ei_hbm, panel.at[0, block], ag0_s.at[4], ag0_r.at[4], to_mate)
+    ag0_f = remote(panel.at[0, far_block], panel.at[0, far_block], ag0_s.at[5], ag0_r.at[5], to_mate)
+    for k in range(3):
+        ag0_x(k).start()
+    ag0_d.start()
+    u0 = remote(eu_hbm, upanel.at[0, ublock], u_s.at[0], u_r.at[0], to_col)
+    u0.start()
+
     rsum[...] = jnp.zeros_like(rsum)
 
     def mask_step(i, carry):
@@ -91,7 +101,7 @@
         def _():
             mask_copy(i + MASK_SLOTS - 1).start()
 
-        cols = pl.ds(pl.multiple_of(i * MASK_COLS, MASK_COLS), MASK_COLS)
+        cols = rows_of(i % 4, i // 4)
         slot = i % MASK_SLOTS
 
         def tile(t, acc):
@@ -99,40 +109,57 @@
             m = mbuf[slot, rows, :].astype(F32)
             adj[rows, cols] = m.astype(BF16)
             part = m[:, 0:128]
-            for g in range(1, MASK_COLS // 128):
+            for g in range(1, CHUNK // 128):
                 part = part + m[:, g * 128:(g + 1) * 128]
             rsum[rows, :] += part
-            return acc + jnp.sum(m.reshape(8, 8, MASK_COLS), axis=0)
-
-        acc = lax.fori_loop(0, users // 64, tile, jnp.zeros((8, MASK_COLS), F32))
-        csum[:, cols] = jnp.sum(acc, axis=0, keepdims=True)
+            return acc + jnp.sum(m.reshape(8, 8, CHUNK), axis=0)
+
+        acc = lax.fori_loop(0, users // 64, tile, jnp.zeros((8, CHUNK), F32))
+        csum[:, pl.ds(pl.multiple_of(i * CHUNK, CHUNK), CHUNK)] = jnp.sum(acc, axis=0, keepdims=True)
         return carry
 
-    lax.fori_loop(0, n_mask, mask_step, 0)
-
-    deg_d = remote(csum, ccore, deg_s.at[0], deg_r.at[0], to_mate)
-    deg_d.start()
+    early = EARLY * 4 * CHUNK
+    parts = (pl.ds(0, early), pl.ds(early, items - early))
+
+    def deg_d(k):
+        return remote(csum.at[:, parts[k]], ccore.at[:, parts[k]], deg_s.at[k], deg_r.at[k], to_mate)
+
+    def deg_x(k):
+        return remote(cchip.at[:, parts[k]], cfar.at[:, parts[k]], deg_s.at[2 + k], deg_r.at[2 + k], to_far)
+
+    def add_core(k):
+        deg_d(k).wait()
+        cchip[:, parts[k]] = csum[:, parts[k]] + ccore[:, parts[k]]
+        deg_x(k).start()
+
+    def col_factors(k):
+        deg_x(k).wait()
+        csum[:, parts[k]] = lax.rsqrt(jnp.maximum(cchip[:, parts[k]] + cfar[:, parts[k]], 1.0))
+
+    lax.fori_loop(0, 4 * EARLY, mask_step, 0)
+    deg_d(0).start()
+    lax.fori_loop(4 * EARLY, 4 * EARLY + 4, mask_step, 0)
+    add_core(0)
+    ag0_x(3).start()
+    lax.fori_loop(4 * EARLY + 4, n_mask, mask_step, 0)
+
     ones = jnp.ones((8, 128), BF16)
     rdeg[...] = lax.dot_general(ones, rsum[...].astype(BF16), (((1,), (1,)), ((), ())),
                                 preferred_element_type=F32)
-    deg_y = remote(rdeg, rdfar, deg_s.at[1], deg_r.at[1], to_col)
+    deg_y = remote(rdeg, rdfar, deg_s.at[4], deg_r.at[4], to_col)
     deg_y.start()
-    deg_d.wait()
-    cchip[...] = csum[...] + ccore[...]
-    deg_x = remote(cchip, cfar, deg_s.at[2], deg_r.at[2], to_far)
-    deg_x.start()
-    ag0_x.wait_recv()
-    ag0_f.start()
+    deg_d(1).start()
+    for copy in inputs:
+        copy.wait()
     u0.wait_recv()
+    col_factors(0)
+    add_core(1)
     deg_y.wait()
     deg_u = jnp.maximum(rdeg[0:1, :] + rdfar[0:1, :], 1.0)
     rscale[...] = lax.rsqrt(jnp.broadcast_to(deg_u, (128, users)).T)
-    deg_x.wait()
-    csum[...] = lax.rsqrt(jnp.maximum(cchip[...] + cfar[...], 1.0))
 
     def scale_block(owner, j):
-        cols = rows_of(owner, j)
-        ci = csum[:, cols]
+        ci = csum[:, pl.ds(pl.multiple_of((j * 4 + owner) * CHUNK, CHUNK), CHUNK)]
 
         def tile(t, carry):
             rows = pl.ds(pl.multiple_of(t * SCALE_ROWS, SCALE_ROWS), SCALE_ROWS)
@@ -379,14 +406,19 @@
         lax.fori_loop(lo, hi, step, 0)
 
     for layer in range(1, NUM_LAYERS + 1):
-        loop(0, n_chunk, functools.partial(item_send_step, layer=layer))
+        if layer == 1:
+            loop(0, EARLY, functools.partial(item_send_step, layer=layer))
+            col_factors(1)
+            for k in range(4):
+                ag0_x(k).wait()
+            ag0_f.start()
+            loop(EARLY, n_chunk, functools.partial(item_send_step, layer=layer))
+        else:
+            loop(0, n_chunk, functools.partial(item_send_step, layer=layer))
         add_mate(n_chunk - 1, layer)
         if layer == 1:
-            ag0_d.wait_recv()
-            ag0_f.wait_recv()
-            ag0_x.wait_send()
-            ag0_d.wait_send()
-            ag0_f.wait_send()
+            ag0_d.wait()
+            ag0_f.wait()
             u0.wait_send()
         else:
             gather_items(layer - 1)
@@ -439,14 +471,9 @@
 
     e_user, e_pos, e_neg = both(0), both(1), both(2)
     prod = e_user * (e_pos - e_neg)
-    dots[0] = jnp.sum(prod.T, axis=0, keepdims=True)
-    dot_copy = remote(dots.at[0], dots.at[1], dot_s.at[0], dot_r.at[0], to_emb)
-    dot_copy.start()
-    dot_copy.wait()
-    z = -(dots[0] + dots[1])
     mine = pl.ds(pl.multiple_of((row * 2 + col) * share, share), share)
-    loss_ref[:, mine] = jnp.maximum(z, 0.0) + jnp.log1p(jnp.exp(-jnp.abs(z)))
-    copies = [remote(loss_ref.at[:, mine], loss_ref.at[:, mine], loss_s.at[k], loss_r.at[k], target)
+    dots[emb, :, mine] = jnp.sum(prod.T, axis=0, keepdims=True)
+    copies = [remote(dots.at[emb, :, mine], dots.at[emb, :, mine], loss_s.at[k], loss_r.at[k], target)
               for k, target in enumerate(peers)]
     for copy in copies:
         copy.start()
@@ -459,6 +486,33 @@
     loop(0, n_chunk, lambda j: out_copy(j).wait())
     for copy in copies:
         copy.wait()
+    z = -(dots[0] + dots[1])
+    loss_ref[...] = jnp.maximum(z, 0.0) + jnp.log1p(jnp.exp(-jnp.abs(z)))
+
+
+def hand_out_kernel(u_in, i_in, l_in, u_out, i_out, l_out, u_buf, i_buf, l_buf, in_s, out_s):
+    pieces = [(u_in, u_buf, u_out), (l_in, l_buf, l_out)]
+    rows = i_in.shape[0] // 4
+    pieces += [tuple(ref.at[pl.ds(k * rows, rows)] for ref in (i_in, i_buf, i_out)) for k in range(4)]
+    for k, (src, buf, dst) in enumerate(pieces):
+        pltpu.make_async_copy(src, buf, in_s.at[k]).start()
+    for k, (src, buf, dst) in enumerate(pieces):
+        pltpu.make_async_copy(src, buf, in_s.at[k]).wait()
+        pltpu.make_async_copy(buf, dst, out_s.at[k]).start()
+    for k, (src, buf, dst) in enumerate(pieces):
+        pltpu.make_async_copy(buf, dst, out_s.at[k]).wait()
+
+
+def hand_out(*arrays):
+    return pl.pallas_call(
+        hand_out_kernel,
+        name="hand_out",
+        out_shape=tuple(jax.ShapeDtypeStruct(a.shape, a.dtype) for a in arrays),
+        in_specs=[pl.BlockSpec(memory_space=pl.ANY)] * 3,
+        out_specs=(pl.BlockSpec(memory_space=pl.ANY),) * 3,
+        scratch_shapes=[*(pltpu.VMEM(a.shape, a.dtype) for a in arrays),
+                        pltpu.SemaphoreType.DMA((6,)), pltpu.SemaphoreType.DMA((6,))],
+    )(*arrays)
 
 
 def propagate(mask_blk, user_sh, item_sh, triples):
@@ -474,13 +528,12 @@
         name="propagate",
         out_shape=(jax.ShapeDtypeStruct((own_u, dim), BF16), jax.ShapeDtypeStruct((own_i, dim), BF16),
                    jax.ShapeDtypeStruct((1, num_trip), F32)),
-        in_specs=[pl.BlockSpec(memory_space=pl.ANY), pl.BlockSpec(memory_space=pltpu.VMEM),
-                  pl.BlockSpec(memory_space=pltpu.VMEM), pl.BlockSpec(memory_space=pltpu.SMEM)],
+        in_specs=[pl.BlockSpec(memory_space=pl.ANY)] * 4,
         out_specs=(pl.BlockSpec(memory_space=pltpu.VMEM), pl.BlockSpec(memory_space=pl.ANY),
                    pl.BlockSpec(memory_space=pltpu.VMEM)),
         scratch_shapes=[
             vmem((users, items), BF16),
-            vmem((MASK_SLOTS, users, MASK_COLS), jnp.int32),
+            vmem((MASK_SLOTS, users, CHUNK), jnp.int32),
             vmem((2, items, dim), BF16),
             vmem((4 * own_i + 8, dim), F32),
             vmem((CORE_SLOTS * 2 * CHUNK + 8, dim), F32),
@@ -488,6 +541,9 @@
             vmem((3, users, dim), BF16),
             vmem((users, dim), F32),
             vmem((3 * own_u, dim), F32),
+            vmem((own_u, dim), BF16),
+            vmem((own_i, dim), BF16),
+            pltpu.SMEM((3, num_trip), jnp.int32),
             vmem((1, items), F32),
             vmem((1, items), F32),
             vmem((1, items), F32),
@@ -496,10 +552,11 @@
             vmem((8, users), F32),
             pltpu.SMEM((6 * share,), jnp.int32),
             vmem((3 * share, dim), BF16),
-            vmem((2, 1, share), F32),
+            vmem((2, 1, num_trip), F32),
+            dma((5,)),
             dma((MASK_SLOTS,)),
-            dma((3,)), dma((3,)),
-            dma((3,)), dma((3,)),
+            dma((6,)), dma((6,)),
+            dma((5,)), dma((5,)),
             dma((3,)), dma((3,)),
             dma((3,)), dma((3,)),
             dma((CORE_SLOTS,)), dma((CORE_SLOTS,)),
@@ -510,9 +567,8 @@
             dma((3, n_chunk)), dma((3, n_chunk)),
             dma((3,)), dma((3,)),
             dma((3,)), dma((3,)),
-            dma((1,)), dma((1,)),
             dma((n_chunk,)),
-            dma((7,)), dma((7,)),
+            dma((15,)), dma((15,)),
         ],
         compiler_params=pltpu.CompilerParams(collective_id=0, has_side_effects=True,
                                              vmem_limit_bytes=67_043_328),
@@ -521,7 +577,7 @@
 
 def solution(mesh):
     def local_fn(mask_blk, user_sh, item_sh, triples):
-        final_user, final_item, loss = propagate(mask_blk, user_sh, item_sh, triples)
+        final_user, final_item, loss = hand_out(*propagate(mask_blk, user_sh, item_sh, triples))
         return final_user, final_item, loss.reshape(-1)
 
     return jax.shard_map(

time: 247 us -> 238 us (0.964)
  local copies, waits for them, and re-layouts: 5.15 us -> 0 us
  Pallas kernels: 241 us -> 237 us
    pallas_call x1, Pallas kernels: 241 us -> 235 us  [propagate(): pl.pallas_call(prop_kernel, name='propagate', out_shape=(jax.ShapeDtypeSt...]
    unnamed x3 -> x0, local copies, waits for them, and re-layouts: 5.15 us -> none
where the time goes in v4:
time: 238 us
  Pallas kernels  237 us (100%)
    pallas_call x1, Pallas kernels, propagate(): pl.pallas_call(prop_kernel, name='propagate', out_shape=(jax.ShapeDtypeSt...  235 us

profile of v4, /device:TPU:0, one launch (start us, length us, event | category | flops | bytes accessed | tf_op | source)
XLA Modules:
  0.0 237.7 jit_solution(7035437065468992464)
XLA Ops:
  0.6 235.0 %propagate.1 = (bf16[512,128]{1,0:T(8,128)(2,1)}, bf16[4096,128]{1,0:T(8,128)(2,1)}, f32[1,4096]{1,0:T(1,128)}) custom-call(s32[1024,16384]{1,0:T(8,128)} %mask_hbm.1, bf16[512,128]{1,0:T(8,128)(2,1)} %eu_hbm.1, bf16[4096,128]{1,0:T(8,128)(2,1)} %ei_hbm.1, s32[3,4096]{1,0:T(4,128)} %bitcast.2), custom_call_target="tpu_custom_call" | custom-call | tf_op jit(solution)/shard_map/propagate/pallas_call | solution.py:526
  235.6 2.1 hand_out.1

commit v5 on v4

--- a/solution.py
+++ b/solution.py
@@ -14,7 +14,8 @@
 
 CHUNK = 256
 MASK_SLOTS = 7
-EARLY = 12
+GROUP = 4
+EARLY = 8
 PIECES = 16
 CORE_SLOTS = 4
 SCALE_ROWS = 256
@@ -23,8 +24,8 @@
 
 
 def prop_kernel(mask_hbm, eu_hbm, ei_hbm, trip_hbm, outu_ref, outi_ref, loss_ref,
-                adj, mbuf, panel, table, stage, drecv, upanel, upart, yflat, eu_ref, ei_ref, trip_ref,
-                csum, ccore, cchip, cfar, rdeg, rdfar, pick_idx, pick_in, dots,
+                adj, mbuf, panel, table, stage, drecv, upanel, upart, yflat, eu_ref, ei_ref, trip_ref, trip_vec,
+                csum, ccore, cchip, cfar, rdeg, rdfar, pick_idx, pick_in, mixed, dots,
                 in_s, msem, ag0_s, ag0_r, deg_s, deg_r, u_s, u_r, y_s, y_r,
                 d_s, d_r, x_s, x_r, agx_s, agx_r, agd_s, agd_r, agf_s, agf_r,
                 fin_s, fin_r, fu_s, fu_r, pick_s, pick_r, out_s, loss_s, loss_r):
@@ -68,29 +69,13 @@
         mask_copy(i).start()
     inputs = [pltpu.make_async_copy(src, dst, in_s.at[k]) for k, (src, dst) in enumerate((
         (eu_hbm, upanel.at[0, ublock]), (ei_hbm, panel.at[0, block]), (eu_hbm, eu_ref), (ei_hbm, ei_ref),
-        (trip_hbm, trip_ref)))]
+        (trip_hbm, trip_ref), (trip_hbm, trip_vec)))]
     for copy in inputs:
         copy.start()
 
     barrier = pltpu.get_barrier_semaphore()
     for target in peers:
         pl.semaphore_signal(barrier, inc=1, device_id=target, device_id_type=MESH)
-    pl.semaphore_wait(barrier, len(peers))
-
-    quarter = own_i // 4
-
-    def ag0_x(k):
-        return remote(ei_hbm.at[pl.ds(k * quarter, quarter)],
-                      panel.at[0, pl.ds(pl.multiple_of(row * own_i + k * quarter, quarter), quarter)],
-                      ag0_s.at[k], ag0_r.at[k], to_far)
-
-    ag0_d = remote(ei_hbm, panel.at[0, block], ag0_s.at[4], ag0_r.at[4], to_mate)
-    ag0_f = remote(panel.at[0, far_block], panel.at[0, far_block], ag0_s.at[5], ag0_r.at[5], to_mate)
-    for k in range(3):
-        ag0_x(k).start()
-    ag0_d.start()
-    u0 = remote(eu_hbm, upanel.at[0, ublock], u_s.at[0], u_r.at[0], to_col)
-    u0.start()
 
     rsum[...] = jnp.zeros_like(rsum)
 
@@ -118,6 +103,23 @@
         csum[:, pl.ds(pl.multiple_of(i * CHUNK, CHUNK), CHUNK)] = jnp.sum(acc, axis=0, keepdims=True)
         return carry
 
+    pl.semaphore_wait(barrier, len(peers))
+
+    quarter = own_i // 4
+
+    def ag0_x(k):
+        return remote(ei_hbm.at[pl.ds(k * quarter, quarter)],
+                      panel.at[0, pl.ds(pl.multiple_of(row * own_i + k * quarter, quarter), quarter)],
+                      ag0_s.at[0], ag0_r.at[0], to_far)
+
+    ag0_d = remote(ei_hbm, panel.at[0, block], ag0_s.at[1], ag0_r.at[1], to_mate)
+    ag0_f = remote(panel.at[0, far_block], panel.at[0, far_block], ag0_s.at[2], ag0_r.at[2], to_mate)
+    for k in range(2):
+        ag0_x(k).start()
+    ag0_d.start()
+    u0 = remote(eu_hbm, upanel.at[0, ublock], u_s.at[0], u_r.at[0], to_col)
+    u0.start()
+
     early = EARLY * 4 * CHUNK
     parts = (pl.ds(0, early), pl.ds(early, items - early))
 
@@ -140,12 +142,13 @@
     deg_d(0).start()
     lax.fori_loop(4 * EARLY, 4 * EARLY + 4, mask_step, 0)
     add_core(0)
+    ag0_x(2).start()
     ag0_x(3).start()
     lax.fori_loop(4 * EARLY + 4, n_mask, mask_step, 0)
 
     ones = jnp.ones((8, 128), BF16)
     rdeg[...] = lax.dot_general(ones, rsum[...].astype(BF16), (((1,), (1,)), ((), ())),
-                                preferred_element_type=F32)
+                                preferred_element_type=F32)[0:1, :]
     deg_y = remote(rdeg, rdfar, deg_s.at[4], deg_r.at[4], to_col)
     deg_y.start()
     deg_d(1).start()
@@ -155,7 +158,7 @@
     col_factors(0)
     add_core(1)
     deg_y.wait()
-    deg_u = jnp.maximum(rdeg[0:1, :] + rdfar[0:1, :], 1.0)
+    deg_u = jnp.maximum(rdeg[...] + rdfar[...], 1.0)
     rscale[...] = lax.rsqrt(jnp.broadcast_to(deg_u, (128, users)).T)
 
     def scale_block(owner, j):
@@ -177,7 +180,8 @@
                                preferred_element_type=F32)
 
     def core_copy(slot):
-        return remote(stage.at[slot_rows(slot)], drecv.at[slot_rows(slot)], d_s.at[slot], d_r.at[slot], to_mate)
+        rows = slot_rows(slot)
+        return remote(stage.at[rows], drecv.at[rows], d_s.at[slot], d_r.at[slot], to_mate)
 
     def region(k, j):
         return pl.ds(pl.multiple_of(k * own_i + j * CHUNK, CHUNK), CHUNK)
@@ -200,7 +204,11 @@
         return pl.ds(pl.multiple_of(slot * 2 * CHUNK + half * CHUNK, CHUNK), CHUNK)
 
     def x_copy(j, layer):
-        return remote(table.at[xsend(j)], table.at[arrived(j, layer)], x_s.at[j], x_r.at[layer % 2, j], to_far)
+        return remote(table.at[xsend(j)], table.at[arrived(j, layer)], x_s.at[j // GROUP], x_r.at[layer % 2, j], to_far)
+
+    def x_sent(g):
+        rows = pl.ds(pl.multiple_of(3 * own_i + g * GROUP * CHUNK, GROUP * CHUNK), GROUP * CHUNK)
+        remote(table.at[rows], table.at[rows], x_s.at[g], x_r.at[0, 0], to_far).wait_send()
 
     def item_send_step(j, layer):
         slot = j % CORE_SLOTS
@@ -212,48 +220,70 @@
             scale_block(mate, j)
         else:
             core_copy(slot).wait_send()
+
+            @pl.when(j % GROUP == 0)
+            def _():
+                x_sent(j // GROUP)
         stage[slot_rows(slot, 0), :] = item_part(far_mate, j, layer)
         stage[slot_rows(slot, 1), :] = item_part(mate, j, layer)
         core_copy(slot).start()
         if layer == 1:
             scale_block(far, j)
             scale_block(row, j)
-        else:
-            x_copy(j, layer - 1).wait_send()
         table[xsend(j), :] = item_part(far, j, layer)
         table[near(j), :] = item_part(row, j, layer)
-
-        @pl.when(j == 0)
-        def _():
-            add_mate(0, layer)
+        if layer > 1:
+            @pl.when(j == 0)
+            def _():
+                add_mate(0, layer)
 
         @pl.when(j >= 2)
         def _():
             add_mate(j - 1, layer)
 
+    def first_send_step():
+        scale_block(far_mate, 0)
+        scale_block(mate, 0)
+        stage[slot_rows(0, 0), :] = item_part(far_mate, 0, 1)
+        stage[slot_rows(0, 1), :] = item_part(mate, 0, 1)
+        core_copy(0).start()
+        scale_block(far, 0)
+        table[xsend(0), :] = item_part(far, 0, 1)
+        add_far(0, 1)
+        scale_block(row, 0)
+        table[near(0), :] = item_part(row, 0, 1)
+        add_near(0)
+
     def add_mate(j, layer):
+        add_far(j, layer)
+        add_near(j)
+
+    def add_far(j, layer):
         slot = j % CORE_SLOTS
         core_copy(slot).wait_recv()
         table[xsend(j), :] += drecv[slot_rows(slot, 0), :]
-        table[near(j), :] += drecv[slot_rows(slot, 1), :]
         x_copy(j, layer).start()
 
-    def ag_copy(kind, j, layer):
+    def add_near(j):
+        table[near(j), :] += drecv[slot_rows(j % CORE_SLOTS, 1), :]
+
+    def ag_copy(kind, g, layer, whole=False):
         par = layer % 2
-        block = panel.at[par, rows_of(far if kind == "fwd" else row, j)]
+        rows = rows_of(far if kind == "fwd" else row, 0 if whole else g, own_i if whole else GROUP * CHUNK)
+        piece = panel.at[par, rows]
         ssem, rsem, target = {"x": (agx_s, agx_r, to_far), "mate": (agd_s, agd_r, to_mate),
                               "fwd": (agf_s, agf_r, to_mate)}[kind]
-        return remote(block, block, ssem.at[j], rsem.at[par, j], target)
+        return remote(piece, piece, ssem.at[0], rsem.at[par, g], target)
 
     def fin_copy(kind, j):
         src, dst, k, target = {
             "col": (panel.at[1, rows_of(row, j)], panel.at[1, rows_of(far, j)], 0, to_col),
             "mate": (panel.at[1, rows_of(row, j)], panel.at[1, rows_of(row, j)], 1, to_mate),
             "fwd": (panel.at[1, rows_of(far, j)], panel.at[1, rows_of(far, j)], 2, to_mate)}[kind]
-        return remote(src, dst, fin_s.at[k, j], fin_r.at[k, j], target)
+        return remote(src, dst, fin_s.at[k], fin_r.at[k, j], target)
 
     def out_copy(j):
-        return pltpu.make_async_copy(panel.at[1, rows_of(row, j)], outi_ref.at[chunk_rows(j)], out_s.at[j])
+        return pltpu.make_async_copy(panel.at[1, rows_of(row, j)], outi_ref.at[chunk_rows(j)], out_s.at[0])
 
     def fin_near(j):
         fin_copy("col", j).wait_recv()
@@ -263,7 +293,10 @@
         table[region(1, j), :] = panel[1, rows_of(mate, j), :].astype(F32)
 
     def fin_fwd(j):
-        x_copy(j, NUM_LAYERS).wait_send()
+        @pl.when(j % GROUP == 0)
+        def _():
+            x_sent(j // GROUP)
+
         fin_copy("fwd", j).wait_recv()
         table[region(3, j), :] = panel[1, rows_of(far_mate, j), :].astype(F32)
 
@@ -273,8 +306,11 @@
         value = (table[near(j), :] + table[arrived(j, layer), :]).astype(BF16)
         if layer < NUM_LAYERS:
             panel[par, rows_of(row, j), :] = value
-            ag_copy("x", j, layer).start()
-            ag_copy("mate", j, layer).start()
+
+            @pl.when(j % GROUP == GROUP - 1)
+            def _():
+                ag_copy("x", j // GROUP, layer).start()
+                ag_copy("mate", j // GROUP, layer).start()
         else:
             total = ei_ref[chunk_rows(j), :].astype(F32) + panel[1, rows_of(row, j), :].astype(F32)
             total = total + panel[0, rows_of(row, j), :].astype(F32)
@@ -287,20 +323,14 @@
             out_copy(j).start()
 
     def gather_items(layer):
-        def forward(j, carry):
-            ag_copy("x", j, layer).wait_recv()
-            ag_copy("fwd", j, layer).start()
-            return carry
-
-        def settle(j, carry):
-            ag_copy("mate", j, layer).wait_recv()
-            ag_copy("fwd", j, layer).wait_recv()
-            for kind in ("x", "mate", "fwd"):
-                ag_copy(kind, j, layer).wait_send()
-            return carry
-
-        lax.fori_loop(0, n_chunk, forward, 0)
-        lax.fori_loop(0, n_chunk, settle, 0)
+        for g in range(n_chunk // GROUP):
+            ag_copy("x", g, layer).wait_recv()
+            ag_copy("fwd", g, layer).start()
+        for g in range(n_chunk // GROUP):
+            ag_copy("mate", g, layer).wait_recv()
+            ag_copy("fwd", g, layer).wait_recv()
+        for kind in ("x", "mate", "fwd"):
+            ag_copy(kind, 0, layer, whole=True).wait_send()
 
     def user_part(layer):
         par = (layer - 1) % 2
@@ -317,10 +347,10 @@
         return pl.ds((layer - 1) * own_u, own_u)
 
     def y_copy(layer):
-        return remote(upart.at[oblock], yflat.at[yrows(layer)], y_s.at[layer - 1], y_r.at[layer - 1], to_col)
+        return remote(upart.at[oblock], yflat.at[yrows(layer)], y_s.at[0], y_r.at[0], to_col)
 
     def u_copy(layer):
-        return remote(upanel.at[layer, ublock], upanel.at[layer, ublock], u_s.at[layer], u_r.at[layer], to_col)
+        return remote(upanel.at[layer, ublock], upanel.at[layer, ublock], u_s.at[0], u_r.at[0], to_col)
 
     def finish_user(layer):
         y_copy(layer).wait()
@@ -333,15 +363,16 @@
             total = total + upanel[2, ublock, :].astype(F32)
             total = total + value.astype(F32)
             final = (total / (NUM_LAYERS + 1)).astype(BF16)
-            outu_ref[...] = final
+            eu_ref[...] = final
+            pltpu.make_async_copy(eu_ref, outu_ref, out_s.at[1]).start()
             stage[0:own_u, :] = final.astype(F32)
             fu_copy("col").start()
             fu_copy("mate").start()
 
     def fu_copy(kind):
         src, dst, k, target = {
-            "col": (outu_ref, upanel.at[0, pl.ds(0, own_u)], 0, to_col),
-            "mate": (outu_ref, upanel.at[0, pl.ds(own_u, own_u)], 1, to_mate),
+            "col": (eu_ref, upanel.at[0, pl.ds(0, own_u)], 0, to_col),
+            "mate": (eu_ref, upanel.at[0, pl.ds(own_u, own_u)], 1, to_mate),
             "fwd": (upanel.at[0, pl.ds(0, own_u)], upanel.at[1, oblock], 2, to_mate)}[kind]
         return remote(src, dst, fu_s.at[k], fu_r.at[k], target)
 
@@ -386,18 +417,29 @@
 
         lax.fori_loop(0, share // 8, step, 0)
 
-    def out_rows(which):
-        return pl.ds(pl.multiple_of(far * own_i + which * share, share), share)
-
-    def pick_copy(which):
-        rows = pl.ds(which * share, share)
-        return remote(panel.at[0, out_rows(which)], pick_in.at[rows], pick_s.at[which], pick_r.at[which], to_far)
-
-    def pick_far(src, which):
-        pick(src, 0, which, yflat)
-        rows = pl.ds(which * share, share)
-        panel[0, out_rows(which), :] = yflat[rows, :].astype(BF16)
-        pick_copy(which).start()
+    def out_rows(at, size):
+        return pl.ds(pl.multiple_of(far * own_i + at * share, share), size * share)
+
+    def pick_copy(k):
+        at, size = ((0, 2), (2, 1))[k]
+        return remote(panel.at[0, out_rows(at, size)], pick_in.at[pl.ds(at * share, size * share)],
+                      pick_s.at[k], pick_r.at[k], to_far)
+
+    def thirds(k):
+        return pl.ds(k * share, share)
+
+    def swap_users():
+        pick(stage, 0, 0, yflat)
+        pick(stage, 1, 0, drecv)
+        panel[0, out_rows(0, 1), :] = yflat[thirds(0), :].astype(BF16)
+        panel[0, out_rows(1, 1), :] = drecv[thirds(0), :].astype(BF16)
+        pick_copy(0).start()
+
+    def mark_mixed():
+        ids = trip_vec[1:3, pl.ds(pl.multiple_of((far * 2 + col) * share, share), share)]
+        sides = lax.bitwise_and(lax.shift_right_logical(ids, 13), 1)
+        flag = jnp.where(sides[0:1] == sides[1:2], 0.0, 1.0)
+        mixed[...] = jnp.broadcast_to(flag, (128, share)).T
 
     def loop(lo, hi, body):
         def step(j, carry):
@@ -407,10 +449,10 @@
 
     for layer in range(1, NUM_LAYERS + 1):
         if layer == 1:
-            loop(0, EARLY, functools.partial(item_send_step, layer=layer))
+            first_send_step()
+            loop(1, EARLY, functools.partial(item_send_step, layer=layer))
             col_factors(1)
-            for k in range(4):
-                ag0_x(k).wait()
+            remote(panel.at[0, far_block], panel.at[0, far_block], ag0_s.at[0], ag0_r.at[0], to_far).wait()
             ag0_f.start()
             loop(EARLY, n_chunk, functools.partial(item_send_step, layer=layer))
         else:
@@ -422,17 +464,27 @@
             u0.wait_send()
         else:
             gather_items(layer - 1)
-        user_part(layer)
-        y_copy(layer).start()
-        if layer < NUM_LAYERS:
-            loop(0, n_chunk // 2, functools.partial(finish_item, layer=layer))
-            if layer == 1:
-                loop(0, 4, place_rows)
+        finish = functools.partial(finish_item, layer=layer)
+        if layer == 1:
+            loop(0, n_chunk // 2, finish)
+            user_part(layer)
+            y_copy(layer).start()
+            loop(n_chunk // 2, n_chunk, finish)
+            loop(0, 4, place_rows)
+            mark_mixed()
             finish_user(layer)
-            if layer > 1:
-                loop(4, PIECES, place_rows)
-            loop(n_chunk // 2, n_chunk, functools.partial(finish_item, layer=layer))
             u_copy(layer).wait()
+        elif layer < NUM_LAYERS:
+            user_part(layer)
+            y_copy(layer).start()
+            loop(0, n_chunk // 2, finish)
+            finish_user(layer)
+            loop(4, PIECES, place_rows)
+            loop(n_chunk // 2, n_chunk, finish)
+            u_copy(layer).wait()
+        else:
+            user_part(layer)
+            y_copy(layer).start()
 
     for slot in range(CORE_SLOTS):
         core_copy(slot).wait_send()
@@ -454,40 +506,51 @@
     finish_user(NUM_LAYERS)
     loop(n_chunk // 2, 3 * n_chunk // 4, last_step)
     gather_users()
-    pick_far(stage, 0)
-    pick(stage, 1, 0, drecv)
+    swap_users()
     loop(3 * n_chunk // 4, n_chunk, last_step)
     loop(n_chunk - LAG, n_chunk, fin_near)
     loop(n_chunk - LAG - 2, n_chunk, fin_fwd)
-    pick_far(table, 1)
-    pick_far(table, 2)
+    pick(table, 0, 1, yflat)
+    pick(table, 0, 2, yflat)
+    diff = yflat[thirds(1), :] - yflat[thirds(2), :]
+    panel[0, out_rows(2, 1), :] = jnp.where(mixed[...] > 0.5, diff, 0.0).astype(BF16)
+    pick_copy(1).start()
     pick(table, 1, 1, drecv)
     pick(table, 1, 2, drecv)
 
-    def both(which):
-        rows = pl.ds(which * share, share)
-        pick_copy(which).wait_recv()
-        return drecv[rows, :] + pick_in[rows, :].astype(F32)
-
-    e_user, e_pos, e_neg = both(0), both(1), both(2)
-    prod = e_user * (e_pos - e_neg)
-    mine = pl.ds(pl.multiple_of((row * 2 + col) * share, share), share)
-    dots[emb, :, mine] = jnp.sum(prod.T, axis=0, keepdims=True)
-    copies = [remote(dots.at[emb, :, mine], dots.at[emb, :, mine], loss_s.at[k], loss_r.at[k], target)
-              for k, target in enumerate(peers)]
-    for copy in copies:
-        copy.start()
-
-    for which in range(3):
-        pick_copy(which).wait_send()
-    for kind in ("col", "mate", "fwd"):
+    def score(user, items_diff):
+        return jnp.sum((user * items_diff).T, axis=0, keepdims=True)
+
+    n_dev = len(peers) + 1
+    base = (emb * (n_dev // 2) + row * 2 + col) * 2 * share
+    pick_copy(0).wait_recv()
+    e_far = yflat[thirds(0), :] + pick_in[thirds(1), :].astype(F32)
+    diff = jnp.where(mixed[...] > 0.5, 0.0, yflat[thirds(1), :] - yflat[thirds(2), :])
+    dots[:, pl.ds(pl.multiple_of(base + share, share), share)] = score(e_far, diff)
+    e_own = drecv[thirds(0), :] + pick_in[thirds(0), :].astype(F32)
+    diff = drecv[thirds(1), :] - drecv[thirds(2), :]
+    pick_copy(1).wait_recv()
+    diff = diff + pick_in[thirds(2), :].astype(F32)
+    dots[:, pl.ds(pl.multiple_of(base, share), share)] = score(e_own, diff)
+    mine = pl.ds(pl.multiple_of(base, 2 * share), 2 * share)
+    for target in peers:
+        remote(dots.at[:, mine], dots.at[:, mine], loss_s.at[0], loss_r.at[0], target).start()
+
+    for k in range(2):
+        pick_copy(k).wait_send()
+    for k, kind in enumerate(("col", "mate", "fwd")):
         fu_copy(kind).wait_send()
-        loop(0, n_chunk, lambda j: fin_copy(kind, j).wait_send())
-    loop(0, n_chunk, lambda j: out_copy(j).wait())
-    for copy in copies:
-        copy.wait()
-    z = -(dots[0] + dots[1])
-    loss_ref[...] = jnp.maximum(z, 0.0) + jnp.log1p(jnp.exp(-jnp.abs(z)))
+        remote(panel.at[1, block], panel.at[1, block], fin_s.at[k], fin_r.at[0, 0], to_mate).wait_send()
+    pltpu.make_async_copy(panel.at[1, block], outi_ref, out_s.at[0]).wait()
+    pltpu.make_async_copy(eu_ref, outu_ref, out_s.at[1]).wait()
+    others = dots.at[:, pl.ds(0, len(peers) * 2 * share)]
+    remote(others, others, loss_s.at[0], loss_r.at[0], to_far).wait()
+    half = n_dev // 2
+    for g in range(half):
+        near_far = [[dots[:, ((e * half + owner) * 2 + k) * share:((e * half + owner) * 2 + k + 1) * share]
+                     for k, owner in ((0, g), (1, (g + half // 2) % half))] for e in range(2)]
+        z = -((near_far[0][0] + near_far[0][1]) + (near_far[1][0] + near_far[1][1]))
+        loss_ref[:, g * share:(g + 1) * share] = jnp.maximum(z, 0.0) + jnp.log1p(jnp.exp(-jnp.abs(z)))
 
 
 def hand_out_kernel(u_in, i_in, l_in, u_out, i_out, l_out, u_buf, i_buf, l_buf, in_s, out_s):
@@ -522,6 +585,7 @@
     n_chunk = own_i // CHUNK
     num_trip = triples.shape[0]
     share = num_trip // 8
+    n_group = n_chunk // GROUP
     vmem, dma = pltpu.VMEM, pltpu.SemaphoreType.DMA
     return pl.pallas_call(
         prop_kernel,
@@ -529,7 +593,7 @@
         out_shape=(jax.ShapeDtypeStruct((own_u, dim), BF16), jax.ShapeDtypeStruct((own_i, dim), BF16),
                    jax.ShapeDtypeStruct((1, num_trip), F32)),
         in_specs=[pl.BlockSpec(memory_space=pl.ANY)] * 4,
-        out_specs=(pl.BlockSpec(memory_space=pltpu.VMEM), pl.BlockSpec(memory_space=pl.ANY),
+        out_specs=(pl.BlockSpec(memory_space=pl.ANY), pl.BlockSpec(memory_space=pl.ANY),
                    pl.BlockSpec(memory_space=pltpu.VMEM)),
         scratch_shapes=[
             vmem((users, items), BF16),
@@ -544,31 +608,32 @@
             vmem((own_u, dim), BF16),
             vmem((own_i, dim), BF16),
             pltpu.SMEM((3, num_trip), jnp.int32),
+            vmem((3, num_trip), jnp.int32),
             vmem((1, items), F32),
             vmem((1, items), F32),
             vmem((1, items), F32),
             vmem((1, items), F32),
-            vmem((8, users), F32),
-            vmem((8, users), F32),
+            vmem((1, users), F32),
+            vmem((1, users), F32),
             pltpu.SMEM((6 * share,), jnp.int32),
             vmem((3 * share, dim), BF16),
-            vmem((2, 1, num_trip), F32),
-            dma((5,)),
-            dma((MASK_SLOTS,)),
-            dma((6,)), dma((6,)),
+            vmem((share, 128), F32),
+            vmem((1, 4 * num_trip), F32),
+            dma((6,)), dma((MASK_SLOTS,)),
+            dma((3,)), dma((3,)),
             dma((5,)), dma((5,)),
+            dma((1,)), dma((1,)),
+            dma((1,)), dma((1,)),
+            dma((CORE_SLOTS,)), dma((CORE_SLOTS,)),
+            dma((n_group,)), dma((2, n_chunk)),
+            dma((1,)), dma((2, n_group)),
+            dma((1,)), dma((2, n_group)),
+            dma((1,)), dma((2, n_group)),
+            dma((3,)), dma((3, n_chunk)),
             dma((3,)), dma((3,)),
-            dma((3,)), dma((3,)),
-            dma((CORE_SLOTS,)), dma((CORE_SLOTS,)),
-            dma((n_chunk,)), dma((2, n_chunk)),
-            dma((n_chunk,)), dma((2, n_chunk)),
-            dma((n_chunk,)), dma((2, n_chunk)),
-            dma((n_chunk,)), dma((2, n_chunk)),
-            dma((3, n_chunk)), dma((3, n_chunk)),
-            dma((3,)), dma((3,)),
-            dma((3,)), dma((3,)),
-            dma((n_chunk,)),
-            dma((15,)), dma((15,)),
+            dma((2,)), dma((2,)),
+            dma((2,)),
+            dma((1,)), dma((1,)),
         ],
         compiler_params=pltpu.CompilerParams(collective_id=0, has_side_effects=True,
                                              vmem_limit_bytes=67_043_328),

time: 238 us -> 235 us (0.987)
  Pallas kernels: 237 us -> 234 us
    pallas_call x1, Pallas kernels: 235 us -> 232 us  [propagate(): pl.pallas_call(prop_kernel, name='propagate', out_shape=(jax.ShapeDtypeSt...]
where the time goes in v5:
time: 235 us
  Pallas kernels  234 us (100%)
    pallas_call x1, Pallas kernels, propagate(): pl.pallas_call(prop_kernel, name='propagate', out_shape=(jax.ShapeDtypeSt...  232 us

profile of v5, /device:TPU:0, one launch (start us, length us, event | category | flops | bytes accessed | tf_op | source)
XLA Modules:
  0.0 234.7 jit_solution(9295561645034533815)
XLA Ops:
  0.6 231.9 %propagate.1 = (bf16[512,128]{1,0:T(8,128)(2,1)}, bf16[4096,128]{1,0:T(8,128)(2,1)}, f32[1,4096]{1,0:T(1,128)}) custom-call(s32[1024,16384]{1,0:T(8,128)} %mask_hbm.1, bf16[512,128]{1,0:T(8,128)(2,1)} %eu_hbm.1, bf16[4096,128]{1,0:T(8,128)(2,1)} %ei_hbm.1, s32[3,4096]{1,0:T(4,128)} %bitcast.2), custom_call_target="tpu_custom_call" | custom-call | tf_op jit(solution)/shard_map/propagate/pallas_call | solution.py:590
  232.6 2.1 hand_out.1

commit v6 on v5

--- a/solution.py
+++ b/solution.py
@@ -179,8 +179,8 @@
         return lax.dot_general(adj[:, rows_of(owner, j)], upanel[layer - 1], (((0,), (0,)), ((), ())),
                                preferred_element_type=F32)
 
-    def core_copy(slot):
-        rows = slot_rows(slot)
+    def core_copy(slot, half=None):
+        rows = slot_rows(slot, half)
         return remote(stage.at[rows], drecv.at[rows], d_s.at[slot], d_r.at[slot], to_mate)
 
     def region(k, j):
@@ -212,60 +212,72 @@
 
     def item_send_step(j, layer):
         slot = j % CORE_SLOTS
-        if layer == 1:
-            @pl.when(j >= CORE_SLOTS)
-            def _():
-                core_copy(slot).wait_send()
-            scale_block(far_mate, j)
-            scale_block(mate, j)
+        if layer == 2:
+            pl.when(j >= CORE_SLOTS)(core_copy(slot).wait_send)
         else:
             core_copy(slot).wait_send()
 
-            @pl.when(j % GROUP == 0)
-            def _():
-                x_sent(j // GROUP)
+        @pl.when(j % GROUP == 0)
+        def _():
+            x_sent(j // GROUP)
+
         stage[slot_rows(slot, 0), :] = item_part(far_mate, j, layer)
         stage[slot_rows(slot, 1), :] = item_part(mate, j, layer)
         core_copy(slot).start()
-        if layer == 1:
-            scale_block(far, j)
-            scale_block(row, j)
         table[xsend(j), :] = item_part(far, j, layer)
         table[near(j), :] = item_part(row, j, layer)
-        if layer > 1:
-            @pl.when(j == 0)
-            def _():
-                add_mate(0, layer)
+
+        @pl.when(j == 0)
+        def _():
+            add_mate(0, layer)
 
         @pl.when(j >= 2)
         def _():
             add_mate(j - 1, layer)
 
-    def first_send_step():
-        scale_block(far_mate, 0)
-        scale_block(mate, 0)
-        stage[slot_rows(0, 0), :] = item_part(far_mate, 0, 1)
-        stage[slot_rows(0, 1), :] = item_part(mate, 0, 1)
-        core_copy(0).start()
-        scale_block(far, 0)
-        table[xsend(0), :] = item_part(far, 0, 1)
-        add_far(0, 1)
-        scale_block(row, 0)
-        table[near(0), :] = item_part(row, 0, 1)
-        add_near(0)
-
     def add_mate(j, layer):
-        add_far(j, layer)
-        add_near(j)
-
-    def add_far(j, layer):
         slot = j % CORE_SLOTS
         core_copy(slot).wait_recv()
         table[xsend(j), :] += drecv[slot_rows(slot, 0), :]
+        table[near(j), :] += drecv[slot_rows(slot, 1), :]
         x_copy(j, layer).start()
 
-    def add_near(j):
-        table[near(j), :] += drecv[slot_rows(j % CORE_SLOTS, 1), :]
+    def layer1_step(j, to_far_chip):
+        slot = j % CORE_SLOTS
+        theirs, ours, here = (far_mate, far, xsend) if to_far_chip else (mate, row, near)
+        if to_far_chip:
+            pl.when(j >= CORE_SLOTS)(core_copy(slot, 0).wait_send)
+        else:
+            core_copy(slot, 0).wait_send()
+        scale_block(theirs, j)
+        scale_block(ours, j)
+        stage[slot_rows(slot, 0), :] = item_part(theirs, j, 1)
+        table[here(j), :] = item_part(ours, j, 1)
+        core_copy(slot, 0).start()
+        if not to_far_chip:
+            @pl.when(j == 0)
+            def _():
+                layer1_add(0, to_far_chip)
+
+        @pl.when(j >= 2)
+        def _():
+            layer1_add(j - 1, to_far_chip)
+
+    def layer1_first():
+        scale_block(far_mate, 0)
+        stage[slot_rows(0, 0), :] = item_part(far_mate, 0, 1)
+        core_copy(0, 0).start()
+        scale_block(far, 0)
+        table[xsend(0), :] = item_part(far, 0, 1)
+        layer1_add(0, True)
+
+    def layer1_add(j, to_far_chip):
+        slot = j % CORE_SLOTS
+        here = xsend if to_far_chip else near
+        core_copy(slot, 0).wait_recv()
+        table[here(j), :] += drecv[slot_rows(slot, 0), :]
+        if to_far_chip:
+            x_copy(j, 1).start()
 
     def ag_copy(kind, g, layer, whole=False):
         par = layer % 2
@@ -408,21 +420,21 @@
 
         lax.fori_loop(piece * (share // PIECES), (piece + 1) * (share // PIECES), step, 0)
 
-    def pick(src, k, which, dst):
+    def pick(src, k, which, dst, lo=0, hi=None):
         def step(t, carry):
             for i in range(8):
                 at = t * 8 + i
                 dst[pl.ds(which * share + at, 1), :] = src[pl.ds(pick_idx[(k * 3 + which) * share + at], 1), :]
             return carry
 
-        lax.fori_loop(0, share // 8, step, 0)
-
-    def out_rows(at, size):
-        return pl.ds(pl.multiple_of(far * own_i + at * share, share), size * share)
+        lax.fori_loop(lo // 8, (hi or share) // 8, step, 0)
+
+    def out_rows(lo, size):
+        return pl.ds(pl.multiple_of(far * own_i + lo, size), size)
 
     def pick_copy(k):
-        at, size = ((0, 2), (2, 1))[k]
-        return remote(panel.at[0, out_rows(at, size)], pick_in.at[pl.ds(at * share, size * share)],
+        lo, size = ((0, 2 * share), (2 * share, share // 2), (5 * share // 2, share // 2))[k]
+        return remote(panel.at[0, out_rows(lo, size)], pick_in.at[pl.ds(lo, size)],
                       pick_s.at[k], pick_r.at[k], to_far)
 
     def thirds(k):
@@ -431,8 +443,8 @@
     def swap_users():
         pick(stage, 0, 0, yflat)
         pick(stage, 1, 0, drecv)
-        panel[0, out_rows(0, 1), :] = yflat[thirds(0), :].astype(BF16)
-        panel[0, out_rows(1, 1), :] = drecv[thirds(0), :].astype(BF16)
+        panel[0, out_rows(0, share), :] = yflat[thirds(0), :].astype(BF16)
+        panel[0, out_rows(share, share), :] = drecv[thirds(0), :].astype(BF16)
         pick_copy(0).start()
 
     def mark_mixed():
@@ -449,15 +461,22 @@
 
     for layer in range(1, NUM_LAYERS + 1):
         if layer == 1:
-            first_send_step()
-            loop(1, EARLY, functools.partial(item_send_step, layer=layer))
+            send_far = functools.partial(layer1_step, to_far_chip=True)
+            send_near = functools.partial(layer1_step, to_far_chip=False)
+            layer1_first()
+            loop(1, EARLY, send_far)
             col_factors(1)
             remote(panel.at[0, far_block], panel.at[0, far_block], ag0_s.at[0], ag0_r.at[0], to_far).wait()
             ag0_f.start()
-            loop(EARLY, n_chunk, functools.partial(item_send_step, layer=layer))
+            loop(EARLY, n_chunk, send_far)
+            layer1_add(n_chunk - 1, True)
+            loop(0, n_chunk, send_near)
+            layer1_add(n_chunk - 1, False)
+            for slot in range(CORE_SLOTS):
+                core_copy(slot, 0).wait_send()
         else:
             loop(0, n_chunk, functools.partial(item_send_step, layer=layer))
-        add_mate(n_chunk - 1, layer)
+            add_mate(n_chunk - 1, layer)
         if layer == 1:
             ag0_d.wait()
             ag0_f.wait()
@@ -510,11 +529,13 @@
     loop(3 * n_chunk // 4, n_chunk, last_step)
     loop(n_chunk - LAG, n_chunk, fin_near)
     loop(n_chunk - LAG - 2, n_chunk, fin_fwd)
-    pick(table, 0, 1, yflat)
-    pick(table, 0, 2, yflat)
-    diff = yflat[thirds(1), :] - yflat[thirds(2), :]
-    panel[0, out_rows(2, 1), :] = jnp.where(mixed[...] > 0.5, diff, 0.0).astype(BF16)
-    pick_copy(1).start()
+    for k in (1, 2):
+        lo, hi = (k - 1) * share // 2, k * share // 2
+        pick(table, 0, 1, yflat, lo, hi)
+        pick(table, 0, 2, yflat, lo, hi)
+        diff = yflat[share + lo:share + hi, :] - yflat[2 * share + lo:2 * share + hi, :]
+        panel[0, out_rows(2 * share + lo, share // 2), :] = jnp.where(mixed[lo:hi, :] > 0.5, diff, 0.0).astype(BF16)
+        pick_copy(k).start()
     pick(table, 1, 1, drecv)
     pick(table, 1, 2, drecv)
 
@@ -530,13 +551,14 @@
     e_own = drecv[thirds(0), :] + pick_in[thirds(0), :].astype(F32)
     diff = drecv[thirds(1), :] - drecv[thirds(2), :]
     pick_copy(1).wait_recv()
+    pick_copy(2).wait_recv()
     diff = diff + pick_in[thirds(2), :].astype(F32)
     dots[:, pl.ds(pl.multiple_of(base, share), share)] = score(e_own, diff)
     mine = pl.ds(pl.multiple_of(base, 2 * share), 2 * share)
     for target in peers:
         remote(dots.at[:, mine], dots.at[:, mine], loss_s.at[0], loss_r.at[0], target).start()
 
-    for k in range(2):
+    for k in range(3):
         pick_copy(k).wait_send()
     for k, kind in enumerate(("col", "mate", "fwd")):
         fu_copy(kind).wait_send()
@@ -631,7 +653,7 @@
             dma((1,)), dma((2, n_group)),
             dma((3,)), dma((3, n_chunk)),
             dma((3,)), dma((3,)),
-            dma((2,)), dma((2,)),
+            dma((3,)), dma((3,)),
             dma((2,)),
             dma((1,)), dma((1,)),
         ],

time: 235 us -> 230 us (0.979)
  Pallas kernels: 234 us -> 229 us
    pallas_call x1, Pallas kernels: 232 us -> 227 us  [propagate(): pl.pallas_call(prop_kernel, name='propagate', out_shape=(jax.ShapeDtypeSt...]
where the time goes in v6:
time: 230 us
  Pallas kernels  229 us (100%)
    pallas_call x1, Pallas kernels, propagate(): pl.pallas_call(prop_kernel, name='propagate', out_shape=(jax.ShapeDtypeSt...  227 us

profile of v6, /device:TPU:0, one launch (start us, length us, event | category | flops | bytes accessed | tf_op | source)
XLA Modules:
  0.0 229.9 jit_solution(8425145143280184933)
XLA Ops:
  0.6 227.2 %propagate.1 = (bf16[512,128]{1,0:T(8,128)(2,1)}, bf16[4096,128]{1,0:T(8,128)(2,1)}, f32[1,4096]{1,0:T(1,128)}) custom-call(s32[1024,16384]{1,0:T(8,128)} %mask_hbm.1, bf16[512,128]{1,0:T(8,128)(2,1)} %eu_hbm.1, bf16[4096,128]{1,0:T(8,128)(2,1)} %ei_hbm.1, s32[3,4096]{1,0:T(4,128)} %bitcast.2), custom_call_target="tpu_custom_call" | custom-call | tf_op jit(solution)/shard_map/propagate/pallas_call | solution.py:612
  227.8 2.1 hand_out.1

commit v7 on v6

--- a/solution.py
+++ b/solution.py
@@ -26,9 +26,9 @@
 def prop_kernel(mask_hbm, eu_hbm, ei_hbm, trip_hbm, outu_ref, outi_ref, loss_ref,
                 adj, mbuf, panel, table, stage, drecv, upanel, upart, yflat, eu_ref, ei_ref, trip_ref, trip_vec,
                 csum, ccore, cchip, cfar, rdeg, rdfar, pick_idx, pick_in, mixed, dots,
-                in_s, msem, ag0_s, ag0_r, deg_s, deg_r, u_s, u_r, y_s, y_r,
+                u_s, u_r, y_s, y_r,
                 d_s, d_r, x_s, x_r, agx_s, agx_r, agd_s, agd_r, agf_s, agf_r,
-                fin_s, fin_r, fu_s, fu_r, pick_s, pick_r, out_s, loss_s, loss_r):
+                fin_s, fin_r, loss_s, loss_r):
     users, items = adj.shape
     rsum = rscale = upart
     own_u = eu_ref.shape[0]
@@ -63,18 +63,19 @@
 
     def mask_copy(i):
         slot = i % MASK_SLOTS
-        return pltpu.make_async_copy(mask_hbm.at[:, rows_of(i % 4, i // 4)], mbuf.at[slot], msem.at[slot])
+        return pltpu.make_async_copy(mask_hbm.at[:, rows_of(i % 4, i // 4)], mbuf.at[slot], fin_r.at[0, slot])
 
     for i in range(MASK_SLOTS - 1):
         mask_copy(i).start()
-    inputs = [pltpu.make_async_copy(src, dst, in_s.at[k]) for k, (src, dst) in enumerate((
+    inputs = [pltpu.make_async_copy(src, dst, fin_r.at[0, 8 + k]) for k, (src, dst) in enumerate((
         (eu_hbm, upanel.at[0, ublock]), (ei_hbm, panel.at[0, block]), (eu_hbm, eu_ref), (ei_hbm, ei_ref),
         (trip_hbm, trip_ref), (trip_hbm, trip_vec)))]
     for copy in inputs:
         copy.start()
 
     barrier = pltpu.get_barrier_semaphore()
-    for target in peers:
+    neighbours = (to_mate, to_far, to_col, {"emb": 1 - emb})
+    for target in neighbours:
         pl.semaphore_signal(barrier, inc=1, device_id=target, device_id_type=MESH)
 
     rsum[...] = jnp.zeros_like(rsum)
@@ -103,17 +104,17 @@
         csum[:, pl.ds(pl.multiple_of(i * CHUNK, CHUNK), CHUNK)] = jnp.sum(acc, axis=0, keepdims=True)
         return carry
 
-    pl.semaphore_wait(barrier, len(peers))
+    pl.semaphore_wait(barrier, len(neighbours))
 
     quarter = own_i // 4
 
     def ag0_x(k):
         return remote(ei_hbm.at[pl.ds(k * quarter, quarter)],
                       panel.at[0, pl.ds(pl.multiple_of(row * own_i + k * quarter, quarter), quarter)],
-                      ag0_s.at[0], ag0_r.at[0], to_far)
-
-    ag0_d = remote(ei_hbm, panel.at[0, block], ag0_s.at[1], ag0_r.at[1], to_mate)
-    ag0_f = remote(panel.at[0, far_block], panel.at[0, far_block], ag0_s.at[2], ag0_r.at[2], to_mate)
+                      fin_r.at[1, 0], fin_r.at[1, 3], to_far)
+
+    ag0_d = remote(ei_hbm, panel.at[0, block], fin_r.at[1, 1], fin_r.at[1, 4], to_mate)
+    ag0_f = remote(panel.at[0, far_block], panel.at[0, far_block], fin_r.at[1, 2], fin_r.at[1, 5], to_mate)
     for k in range(2):
         ag0_x(k).start()
     ag0_d.start()
@@ -124,10 +125,10 @@
     parts = (pl.ds(0, early), pl.ds(early, items - early))
 
     def deg_d(k):
-        return remote(csum.at[:, parts[k]], ccore.at[:, parts[k]], deg_s.at[k], deg_r.at[k], to_mate)
+        return remote(csum.at[:, parts[k]], ccore.at[:, parts[k]], fin_r.at[1, 6 + k], fin_r.at[2, k], to_mate)
 
     def deg_x(k):
-        return remote(cchip.at[:, parts[k]], cfar.at[:, parts[k]], deg_s.at[2 + k], deg_r.at[2 + k], to_far)
+        return remote(cchip.at[:, parts[k]], cfar.at[:, parts[k]], fin_r.at[1, 8 + k], fin_r.at[2, 2 + k], to_far)
 
     def add_core(k):
         deg_d(k).wait()
@@ -149,7 +150,7 @@
     ones = jnp.ones((8, 128), BF16)
     rdeg[...] = lax.dot_general(ones, rsum[...].astype(BF16), (((1,), (1,)), ((), ())),
                                 preferred_element_type=F32)[0:1, :]
-    deg_y = remote(rdeg, rdfar, deg_s.at[4], deg_r.at[4], to_col)
+    deg_y = remote(rdeg, rdfar, fin_r.at[1, 10], fin_r.at[2, 4], to_col)
     deg_y.start()
     deg_d(1).start()
     for copy in inputs:
@@ -294,9 +295,6 @@
             "fwd": (panel.at[1, rows_of(far, j)], panel.at[1, rows_of(far, j)], 2, to_mate)}[kind]
         return remote(src, dst, fin_s.at[k], fin_r.at[k, j], target)
 
-    def out_copy(j):
-        return pltpu.make_async_copy(panel.at[1, rows_of(row, j)], outi_ref.at[chunk_rows(j)], out_s.at[0])
-
     def fin_near(j):
         fin_copy("col", j).wait_recv()
         fin_copy("fwd", j).start()
@@ -329,10 +327,10 @@
             total = total + value.astype(F32)
             final = (total / (NUM_LAYERS + 1)).astype(BF16)
             panel[1, rows_of(row, j), :] = final
+            outi_ref[chunk_rows(j), :] = final
             table[near(j), :] = final.astype(F32)
             fin_copy("col", j).start()
             fin_copy("mate", j).start()
-            out_copy(j).start()
 
     def gather_items(layer):
         for g in range(n_chunk // GROUP):
@@ -376,7 +374,7 @@
             total = total + value.astype(F32)
             final = (total / (NUM_LAYERS + 1)).astype(BF16)
             eu_ref[...] = final
-            pltpu.make_async_copy(eu_ref, outu_ref, out_s.at[1]).start()
+            outu_ref[...] = final
             stage[0:own_u, :] = final.astype(F32)
             fu_copy("col").start()
             fu_copy("mate").start()
@@ -386,7 +384,7 @@
             "col": (eu_ref, upanel.at[0, pl.ds(0, own_u)], 0, to_col),
             "mate": (eu_ref, upanel.at[0, pl.ds(own_u, own_u)], 1, to_mate),
             "fwd": (upanel.at[0, pl.ds(0, own_u)], upanel.at[1, oblock], 2, to_mate)}[kind]
-        return remote(src, dst, fu_s.at[k], fu_r.at[k], target)
+        return remote(src, dst, agd_r.at[0, k], agd_r.at[1, k], target)
 
     def gather_users():
         fu_copy("col").wait_recv()
@@ -435,7 +433,7 @@
     def pick_copy(k):
         lo, size = ((0, 2 * share), (2 * share, share // 2), (5 * share // 2, share // 2))[k]
         return remote(panel.at[0, out_rows(lo, size)], pick_in.at[pl.ds(lo, size)],
-                      pick_s.at[k], pick_r.at[k], to_far)
+                      agx_r.at[0, k], agx_r.at[1, k], to_far)
 
     def thirds(k):
         return pl.ds(k * share, share)
@@ -466,7 +464,7 @@
             layer1_first()
             loop(1, EARLY, send_far)
             col_factors(1)
-            remote(panel.at[0, far_block], panel.at[0, far_block], ag0_s.at[0], ag0_r.at[0], to_far).wait()
+            remote(panel.at[0, far_block], panel.at[0, far_block], fin_r.at[1, 0], fin_r.at[1, 3], to_far).wait()
             ag0_f.start()
             loop(EARLY, n_chunk, send_far)
             layer1_add(n_chunk - 1, True)
@@ -563,8 +561,6 @@
     for k, kind in enumerate(("col", "mate", "fwd")):
         fu_copy(kind).wait_send()
         remote(panel.at[1, block], panel.at[1, block], fin_s.at[k], fin_r.at[0, 0], to_mate).wait_send()
-    pltpu.make_async_copy(panel.at[1, block], outi_ref, out_s.at[0]).wait()
-    pltpu.make_async_copy(eu_ref, outu_ref, out_s.at[1]).wait()
     others = dots.at[:, pl.ds(0, len(peers) * 2 * share)]
     remote(others, others, loss_s.at[0], loss_r.at[0], to_far).wait()
     half = n_dev // 2
@@ -575,17 +571,13 @@
         loss_ref[:, g * share:(g + 1) * share] = jnp.maximum(z, 0.0) + jnp.log1p(jnp.exp(-jnp.abs(z)))
 
 
-def hand_out_kernel(u_in, i_in, l_in, u_out, i_out, l_out, u_buf, i_buf, l_buf, in_s, out_s):
-    pieces = [(u_in, u_buf, u_out), (l_in, l_buf, l_out)]
-    rows = i_in.shape[0] // 4
-    pieces += [tuple(ref.at[pl.ds(k * rows, rows)] for ref in (i_in, i_buf, i_out)) for k in range(4)]
-    for k, (src, buf, dst) in enumerate(pieces):
-        pltpu.make_async_copy(src, buf, in_s.at[k]).start()
-    for k, (src, buf, dst) in enumerate(pieces):
-        pltpu.make_async_copy(src, buf, in_s.at[k]).wait()
-        pltpu.make_async_copy(buf, dst, out_s.at[k]).start()
-    for k, (src, buf, dst) in enumerate(pieces):
-        pltpu.make_async_copy(buf, dst, out_s.at[k]).wait()
+def hand_out_kernel(u_in, i_in, l_in, u_out, i_out, l_out, out_s):
+    pieces = [pltpu.make_async_copy(src, dst, out_s.at[k])
+              for k, (src, dst) in enumerate(((i_in, i_out), (u_in, u_out), (l_in, l_out)))]
+    for piece in pieces:
+        piece.start()
+    for piece in pieces:
+        piece.wait()
 
 
 def hand_out(*arrays):
@@ -593,10 +585,10 @@
         hand_out_kernel,
         name="hand_out",
         out_shape=tuple(jax.ShapeDtypeStruct(a.shape, a.dtype) for a in arrays),
-        in_specs=[pl.BlockSpec(memory_space=pl.ANY)] * 3,
+        in_specs=[pl.BlockSpec(memory_space=pltpu.VMEM)] * 3,
         out_specs=(pl.BlockSpec(memory_space=pl.ANY),) * 3,
-        scratch_shapes=[*(pltpu.VMEM(a.shape, a.dtype) for a in arrays),
-                        pltpu.SemaphoreType.DMA((6,)), pltpu.SemaphoreType.DMA((6,))],
+        scratch_shapes=[pltpu.SemaphoreType.DMA((6,))],
+        compiler_params=pltpu.CompilerParams(vmem_limit_bytes=2 * 2 ** 20),
     )(*arrays)
 
 
@@ -612,11 +604,9 @@
     return pl.pallas_call(
         prop_kernel,
         name="propagate",
-        out_shape=(jax.ShapeDtypeStruct((own_u, dim), BF16), jax.ShapeDtypeStruct((own_i, dim), BF16),
-                   jax.ShapeDtypeStruct((1, num_trip), F32)),
+        out_shape=(vmem((own_u, dim), BF16), vmem((own_i, dim), BF16), vmem((1, num_trip), F32)),
         in_specs=[pl.BlockSpec(memory_space=pl.ANY)] * 4,
-        out_specs=(pl.BlockSpec(memory_space=pl.ANY), pl.BlockSpec(memory_space=pl.ANY),
-                   pl.BlockSpec(memory_space=pltpu.VMEM)),
+        out_specs=(pl.BlockSpec(memory_space=pltpu.VMEM),) * 3,
         scratch_shapes=[
             vmem((users, items), BF16),
             vmem((MASK_SLOTS, users, CHUNK), jnp.int32),
@@ -641,9 +631,6 @@
             vmem((3 * share, dim), BF16),
             vmem((share, 128), F32),
             vmem((1, 4 * num_trip), F32),
-            dma((6,)), dma((MASK_SLOTS,)),
-            dma((3,)), dma((3,)),
-            dma((5,)), dma((5,)),
             dma((1,)), dma((1,)),
             dma((1,)), dma((1,)),
             dma((CORE_SLOTS,)), dma((CORE_SLOTS,)),
@@ -652,13 +639,10 @@
             dma((1,)), dma((2, n_group)),
             dma((1,)), dma((2, n_group)),
             dma((3,)), dma((3, n_chunk)),
-            dma((3,)), dma((3,)),
-            dma((3,)), dma((3,)),
-            dma((2,)),
             dma((1,)), dma((1,)),
         ],
         compiler_params=pltpu.CompilerParams(collective_id=0, has_side_effects=True,
-                                             vmem_limit_bytes=67_043_328),
+                                             vmem_limit_bytes=65_700_000),
     )(mask_blk, user_sh, item_sh, triples.T)
 
 

time: 230 us -> 228 us (level)
  no operation moved by 1% of the time
where the time goes in v7:
time: 228 us
  Pallas kernels  227 us (100%)
    pallas_call x1, Pallas kernels, propagate(): pl.pallas_call(prop_kernel, name='propagate', out_shape=(vmem((own_u, dim...  226 us

profile of v7, /device:TPU:0, one launch (start us, length us, event | category | flops | bytes accessed | tf_op | source)
XLA Modules:
  0.0 227.9 jit_solution(15534143134979315185)
XLA Ops:
  0.6 226.2 %propagate.1 = (bf16[512,128]{1,0:T(8,128)(2,1)S(1)}, bf16[4096,128]{1,0:T(8,128)(2,1)S(1)}, f32[1,4096]{1,0:T(1,128)S(1)}) custom-call(s32[1024,16384]{1,0:T(8,128)} %mask_hbm.1, bf16[512,128]{1,0:T(8,128)(2,1)} %eu_hbm.1, bf16[4096,128]{1,0:T(8,128)(2,1)} %ei_hbm.1, s32[3,4096]{1,0:T(4,128)} %bitcast.2), custom_call_target="tpu_custom_call" | custom-call | tf_op jit(solution)/shard_map/propagate/pallas_call | solution.py:604
  226.8 1.1 hand_out.1

commit v8 on v7

--- a/solution.py
+++ b/solution.py
@@ -25,7 +25,7 @@
 
 def prop_kernel(mask_hbm, eu_hbm, ei_hbm, trip_hbm, outu_ref, outi_ref, loss_ref,
                 adj, mbuf, panel, table, stage, drecv, upanel, upart, yflat, eu_ref, ei_ref, trip_ref, trip_vec,
-                csum, ccore, cchip, cfar, rdeg, rdfar, pick_idx, pick_in, mixed, dots,
+                csum, ccore, cchip, cfar, rdeg, rdfar, rdemb, pick_idx, pick_in, mixed, dots,
                 u_s, u_r, y_s, y_r,
                 d_s, d_r, x_s, x_r, agx_s, agx_r, agd_s, agd_r, agf_s, agf_r,
                 fin_s, fin_r, loss_s, loss_r):
@@ -61,9 +61,13 @@
     oblock = pl.ds(pl.multiple_of(other_col * own_u, own_u), own_u)
     n_mask = items // CHUNK
 
+    def mask_block(i):
+        return (i + emb * (n_mask // 2)) % n_mask
+
     def mask_copy(i):
         slot = i % MASK_SLOTS
-        return pltpu.make_async_copy(mask_hbm.at[:, rows_of(i % 4, i // 4)], mbuf.at[slot], fin_r.at[0, slot])
+        b = mask_block(i)
+        return pltpu.make_async_copy(mask_hbm.at[:, rows_of(b % 4, b // 4)], mbuf.at[slot], fin_r.at[0, slot])
 
     for i in range(MASK_SLOTS - 1):
         mask_copy(i).start()
@@ -80,87 +84,98 @@
 
     rsum[...] = jnp.zeros_like(rsum)
 
-    def mask_step(i, carry):
+    def mask_step(i, carry, count):
         mask_copy(i).wait()
 
         @pl.when(i + MASK_SLOTS - 1 < n_mask)
         def _():
             mask_copy(i + MASK_SLOTS - 1).start()
 
-        cols = rows_of(i % 4, i // 4)
+        b = mask_block(i)
+        cols = rows_of(b % 4, b // 4)
         slot = i % MASK_SLOTS
 
         def tile(t, acc):
             rows = pl.ds(pl.multiple_of(t * 64, 64), 64)
             m = mbuf[slot, rows, :].astype(F32)
             adj[rows, cols] = m.astype(BF16)
+            if not count:
+                return acc
             part = m[:, 0:128]
             for g in range(1, CHUNK // 128):
                 part = part + m[:, g * 128:(g + 1) * 128]
             rsum[rows, :] += part
             return acc + jnp.sum(m.reshape(8, 8, CHUNK), axis=0)
 
-        acc = lax.fori_loop(0, users // 64, tile, jnp.zeros((8, CHUNK), F32))
-        csum[:, pl.ds(pl.multiple_of(i * CHUNK, CHUNK), CHUNK)] = jnp.sum(acc, axis=0, keepdims=True)
+        if count:
+            acc = lax.fori_loop(0, users // 64, tile, jnp.zeros((8, CHUNK), F32))
+            csum[:, pl.ds(pl.multiple_of(b * CHUNK, CHUNK), CHUNK)] = jnp.sum(acc, axis=0, keepdims=True)
+        else:
+            lax.fori_loop(0, users // 64, tile, 0)
         return carry
 
+    def stream(lo, hi, count=False):
+        lax.fori_loop(lo, hi, functools.partial(mask_step, count=count), 0)
+
     pl.semaphore_wait(barrier, len(neighbours))
+
+    def head(k):
+        return fin_r.at[1, k], fin_r.at[2, k]
 
     quarter = own_i // 4
 
     def ag0_x(k):
         return remote(ei_hbm.at[pl.ds(k * quarter, quarter)],
                       panel.at[0, pl.ds(pl.multiple_of(row * own_i + k * quarter, quarter), quarter)],
-                      fin_r.at[1, 0], fin_r.at[1, 3], to_far)
-
-    ag0_d = remote(ei_hbm, panel.at[0, block], fin_r.at[1, 1], fin_r.at[1, 4], to_mate)
-    ag0_f = remote(panel.at[0, far_block], panel.at[0, far_block], fin_r.at[1, 2], fin_r.at[1, 5], to_mate)
+                      *head(0), to_far)
+
+    ag0_d = remote(ei_hbm, panel.at[0, block], *head(1), to_mate)
+    ag0_f = remote(panel.at[0, far_block], panel.at[0, far_block], *head(2), to_mate)
     for k in range(2):
         ag0_x(k).start()
     ag0_d.start()
     u0 = remote(eu_hbm, upanel.at[0, ublock], u_s.at[0], u_r.at[0], to_col)
     u0.start()
 
-    early = EARLY * 4 * CHUNK
-    parts = (pl.ds(0, early), pl.ds(early, items - early))
-
-    def deg_d(k):
-        return remote(csum.at[:, parts[k]], ccore.at[:, parts[k]], fin_r.at[1, 6 + k], fin_r.at[2, k], to_mate)
-
-    def deg_x(k):
-        return remote(cchip.at[:, parts[k]], cfar.at[:, parts[k]], fin_r.at[1, 8 + k], fin_r.at[2, 2 + k], to_far)
-
-    def add_core(k):
-        deg_d(k).wait()
-        cchip[:, parts[k]] = csum[:, parts[k]] + ccore[:, parts[k]]
-        deg_x(k).start()
-
-    def col_factors(k):
-        deg_x(k).wait()
-        csum[:, parts[k]] = lax.rsqrt(jnp.maximum(cchip[:, parts[k]] + cfar[:, parts[k]], 1.0))
-
-    lax.fori_loop(0, 4 * EARLY, mask_step, 0)
-    deg_d(0).start()
-    lax.fori_loop(4 * EARLY, 4 * EARLY + 4, mask_step, 0)
-    add_core(0)
+    half_cols = pl.ds(pl.multiple_of(emb * (items // 2), items // 2), items // 2)
+    to_emb = {"emb": 1 - emb}
+    ones = jnp.ones((8, 128), BF16)
+    deg_z = remote(rdeg, rdemb, *head(3), to_emb)
+    deg_y = remote(rdeg, rdfar, *head(4), to_col)
+    deg_d = remote(csum.at[:, half_cols], ccore.at[:, half_cols], *head(5), to_mate)
+    deg_x = remote(cchip.at[:, half_cols], cfar.at[:, half_cols], *head(6), to_far)
+    deg_e = remote(csum.at[:, half_cols], csum.at[:, half_cols], *head(7), to_emb)
+    mid = n_mask // 2
+
+    stream(0, mid, count=True)
+    rdeg[...] = lax.dot_general(ones, rsum[...].astype(BF16), (((1,), (1,)), ((), ())),
+                                preferred_element_type=F32)[0:1, :]
+    deg_z.start()
+    deg_d.start()
+    stream(mid, mid + 5)
+    deg_z.wait()
+    rdeg[...] += rdemb[...]
+    deg_y.start()
+    deg_d.wait()
+    cchip[:, half_cols] = csum[:, half_cols] + ccore[:, half_cols]
+    deg_x.start()
     ag0_x(2).start()
     ag0_x(3).start()
-    lax.fori_loop(4 * EARLY + 4, n_mask, mask_step, 0)
-
-    ones = jnp.ones((8, 128), BF16)
-    rdeg[...] = lax.dot_general(ones, rsum[...].astype(BF16), (((1,), (1,)), ((), ())),
-                                preferred_element_type=F32)[0:1, :]
-    deg_y = remote(rdeg, rdfar, fin_r.at[1, 10], fin_r.at[2, 4], to_col)
-    deg_y.start()
-    deg_d(1).start()
+    stream(mid + 5, mid + 12)
+    deg_y.wait()
+    deg_u = jnp.maximum(rdeg[...] + rdfar[...], 1.0)
+    rscale[...] = lax.rsqrt(jnp.broadcast_to(deg_u, (128, users)).T)
+    stream(mid + 12, mid + 18)
+    deg_x.wait()
+    csum[:, half_cols] = cchip[:, half_cols] + cfar[:, half_cols]
+    deg_e.start()
+    stream(mid + 18, mid + 26)
+    deg_e.wait()
+    csum[...] = lax.rsqrt(jnp.maximum(csum[...], 1.0))
+    stream(mid + 26, n_mask)
     for copy in inputs:
         copy.wait()
     u0.wait_recv()
-    col_factors(0)
-    add_core(1)
-    deg_y.wait()
-    deg_u = jnp.maximum(rdeg[...] + rdfar[...], 1.0)
-    rscale[...] = lax.rsqrt(jnp.broadcast_to(deg_u, (128, users)).T)
 
     def scale_block(owner, j):
         ci = csum[:, pl.ds(pl.multiple_of((j * 4 + owner) * CHUNK, CHUNK), CHUNK)]
@@ -463,8 +478,7 @@
             send_near = functools.partial(layer1_step, to_far_chip=False)
             layer1_first()
             loop(1, EARLY, send_far)
-            col_factors(1)
-            remote(panel.at[0, far_block], panel.at[0, far_block], fin_r.at[1, 0], fin_r.at[1, 3], to_far).wait()
+            remote(panel.at[0, far_block], panel.at[0, far_block], *head(0), to_far).wait()
             ag0_f.start()
             loop(EARLY, n_chunk, send_far)
             layer1_add(n_chunk - 1, True)
@@ -564,10 +578,12 @@
     others = dots.at[:, pl.ds(0, len(peers) * 2 * share)]
     remote(others, others, loss_s.at[0], loss_r.at[0], to_far).wait()
     half = n_dev // 2
+    def scores(e, owner, k):
+        at = ((e * half + owner) * 2 + k) * share
+        return dots[:, at:at + share]
+
     for g in range(half):
-        near_far = [[dots[:, ((e * half + owner) * 2 + k) * share:((e * half + owner) * 2 + k + 1) * share]
-                     for k, owner in ((0, g), (1, (g + half // 2) % half))] for e in range(2)]
-        z = -((near_far[0][0] + near_far[0][1]) + (near_far[1][0] + near_far[1][1]))
+        z = -sum(scores(e, g, 0) + scores(e, (g + half // 2) % half, 1) for e in range(2))
         loss_ref[:, g * share:(g + 1) * share] = jnp.maximum(z, 0.0) + jnp.log1p(jnp.exp(-jnp.abs(z)))
 
 
@@ -601,6 +617,7 @@
     share = num_trip // 8
     n_group = n_chunk // GROUP
     vmem, dma = pltpu.VMEM, pltpu.SemaphoreType.DMA
+    one = dma((1,))
     return pl.pallas_call(
         prop_kernel,
         name="propagate",
@@ -627,19 +644,20 @@
             vmem((1, items), F32),
             vmem((1, users), F32),
             vmem((1, users), F32),
+            vmem((1, users), F32),
             pltpu.SMEM((6 * share,), jnp.int32),
             vmem((3 * share, dim), BF16),
             vmem((share, 128), F32),
             vmem((1, 4 * num_trip), F32),
-            dma((1,)), dma((1,)),
-            dma((1,)), dma((1,)),
+            one, one,
+            one, one,
             dma((CORE_SLOTS,)), dma((CORE_SLOTS,)),
             dma((n_group,)), dma((2, n_chunk)),
-            dma((1,)), dma((2, n_group)),
-            dma((1,)), dma((2, n_group)),
-            dma((1,)), dma((2, n_group)),
+            one, dma((2, n_group)),
+            one, dma((2, n_group)),
+            one, dma((2, n_group)),
             dma((3,)), dma((3, n_chunk)),
-            dma((1,)), dma((1,)),
+            one, one,
         ],
         compiler_params=pltpu.CompilerParams(collective_id=0, has_side_effects=True,
                                              vmem_limit_bytes=65_700_000),

time: 228 us -> 227 us (level)
  no operation moved by 1% of the time
where the time goes in v8:
time: 227 us
  Pallas kernels  226 us (100%)
    pallas_call x1, Pallas kernels, propagate(): pl.pallas_call(prop_kernel, name='propagate', out_shape=(vmem((own_u, dim...  225 us

profile of v8, /device:TPU:0, one launch (start us, length us, event | category | flops | bytes accessed | tf_op | source)
XLA Modules:
  0.0 226.9 jit_solution(5933115756058345760)
XLA Ops:
  0.6 225.2 %propagate.1 = (bf16[512,128]{1,0:T(8,128)(2,1)S(1)}, bf16[4096,128]{1,0:T(8,128)(2,1)S(1)}, f32[1,4096]{1,0:T(1,128)S(1)}) custom-call(s32[1024,16384]{1,0:T(8,128)} %mask_hbm.1, bf16[512,128]{1,0:T(8,128)(2,1)} %eu_hbm.1, bf16[4096,128]{1,0:T(8,128)(2,1)} %ei_hbm.1, s32[3,4096]{1,0:T(4,128)} %bitcast.2), custom_call_target="tpu_custom_call" | custom-call | tf_op jit(solution)/shard_map/propagate/pallas_call | solution.py:621
  225.8 1.1 hand_out.1

commit v9 on v8

--- a/solution.py
+++ b/solution.py
@@ -28,12 +28,13 @@
                 csum, ccore, cchip, cfar, rdeg, rdfar, rdemb, pick_idx, pick_in, mixed, dots,
                 u_s, u_r, y_s, y_r,
                 d_s, d_r, x_s, x_r, agx_s, agx_r, agd_s, agd_r, agf_s, agf_r,
-                fin_s, fin_r, loss_s, loss_r):
+                fin_s, fin_r, half_r, loss_s, loss_r):
     users, items = adj.shape
     rsum = rscale = upart
     own_u = eu_ref.shape[0]
     own_i = ei_ref.shape[0]
     n_chunk = own_i // CHUNK
+    halves = [(k, CHUNK // 2) for k in (2 * n_chunk - 2, 2 * n_chunk - 1)]
     row = lax.axis_index("row")
     col = lax.axis_index("col")
     mate = row + 1 - 2 * (row % 2)
@@ -199,28 +200,31 @@
         rows = slot_rows(slot, half)
         return remote(stage.at[rows], drecv.at[rows], d_s.at[slot], d_r.at[slot], to_mate)
 
-    def region(k, j):
-        return pl.ds(pl.multiple_of(k * own_i + j * CHUNK, CHUNK), CHUNK)
-
-    def near(j):
-        return region(0, j)
-
-    def arrived(j, layer):
-        return region(1 + layer % 2, j)
-
-    def xsend(j):
-        return region(3, j)
-
-    def chunk_rows(j):
-        return pl.ds(pl.multiple_of(j * CHUNK, CHUNK), CHUNK)
+    def region(k, j, size=CHUNK):
+        return pl.ds(pl.multiple_of(k * own_i + j * size, size), size)
+
+    def near(j, size=CHUNK):
+        return region(0, j, size)
+
+    def arrived(j, layer, size=CHUNK):
+        return region(1 + layer % 2, j, size)
+
+    def xsend(j, size=CHUNK):
+        return region(3, j, size)
+
+    def arrival(pool, row_at, j, size, k):
+        if size == CHUNK:
+            return pool.at[row_at, j]
+        return half_r.at[k] if j % 2 else pool.at[row_at, j // 2]
 
     def slot_rows(slot, half=None):
         if half is None:
             return pl.ds(pl.multiple_of(slot * 2 * CHUNK, 2 * CHUNK), 2 * CHUNK)
         return pl.ds(pl.multiple_of(slot * 2 * CHUNK + half * CHUNK, CHUNK), CHUNK)
 
-    def x_copy(j, layer):
-        return remote(table.at[xsend(j)], table.at[arrived(j, layer)], x_s.at[j // GROUP], x_r.at[layer % 2, j], to_far)
+    def x_copy(j, layer, size=CHUNK):
+        return remote(table.at[xsend(j, size)], table.at[arrived(j, layer, size)],
+                      x_s.at[j * size // (GROUP * CHUNK)], arrival(x_r, layer % 2, j, size, 3), to_far)
 
     def x_sent(g):
         rows = pl.ds(pl.multiple_of(3 * own_i + g * GROUP * CHUNK, GROUP * CHUNK), GROUP * CHUNK)
@@ -251,12 +255,14 @@
         def _():
             add_mate(j - 1, layer)
 
-    def add_mate(j, layer):
+    def add_mate(j, layer, parts=None):
+        parts = parts or [(j, CHUNK)]
         slot = j % CORE_SLOTS
         core_copy(slot).wait_recv()
         table[xsend(j), :] += drecv[slot_rows(slot, 0), :]
         table[near(j), :] += drecv[slot_rows(slot, 1), :]
-        x_copy(j, layer).start()
+        for part, size in parts:
+            x_copy(part, layer, size).start()
 
     def layer1_step(j, to_far_chip):
         slot = j % CORE_SLOTS
@@ -303,49 +309,51 @@
                               "fwd": (agf_s, agf_r, to_mate)}[kind]
         return remote(piece, piece, ssem.at[0], rsem.at[par, g], target)
 
-    def fin_copy(kind, j):
-        src, dst, k, target = {
-            "col": (panel.at[1, rows_of(row, j)], panel.at[1, rows_of(far, j)], 0, to_col),
-            "mate": (panel.at[1, rows_of(row, j)], panel.at[1, rows_of(row, j)], 1, to_mate),
-            "fwd": (panel.at[1, rows_of(far, j)], panel.at[1, rows_of(far, j)], 2, to_mate)}[kind]
-        return remote(src, dst, fin_s.at[k], fin_r.at[k, j], target)
-
-    def fin_near(j):
-        fin_copy("col", j).wait_recv()
-        fin_copy("fwd", j).start()
-        table[region(2, j), :] = panel[1, rows_of(far, j), :].astype(F32)
-        fin_copy("mate", j).wait_recv()
-        table[region(1, j), :] = panel[1, rows_of(mate, j), :].astype(F32)
-
-    def fin_fwd(j):
-        @pl.when(j % GROUP == 0)
-        def _():
-            x_sent(j // GROUP)
-
-        fin_copy("fwd", j).wait_recv()
-        table[region(3, j), :] = panel[1, rows_of(far_mate, j), :].astype(F32)
-
-    def finish_item(j, layer):
-        x_copy(j, layer).wait_recv()
+    def fin_copy(kind, j, size=CHUNK):
+        mine, other = panel.at[1, rows_of(row, j, size)], panel.at[1, rows_of(far, j, size)]
+        src, dst, k, target = {"col": (mine, other, 0, to_col), "mate": (mine, mine, 1, to_mate),
+                               "fwd": (other, other, 2, to_mate)}[kind]
+        return remote(src, dst, fin_s.at[k], arrival(fin_r, k, j, size, k), target)
+
+    def fin_near(j, size=CHUNK):
+        fin_copy("col", j, size).wait_recv()
+        fin_copy("fwd", j, size).start()
+        table[region(2, j, size), :] = panel[1, rows_of(far, j, size), :].astype(F32)
+        fin_copy("mate", j, size).wait_recv()
+        table[region(1, j, size), :] = panel[1, rows_of(mate, j, size), :].astype(F32)
+
+    def fin_fwd(j, size=CHUNK):
+        if size == CHUNK:
+            @pl.when(j % GROUP == 0)
+            def _():
+                x_sent(j // GROUP)
+
+        fin_copy("fwd", j, size).wait_recv()
+        table[region(3, j, size), :] = panel[1, rows_of(far_mate, j, size), :].astype(F32)
+
+    def finish_item(j, layer, size=CHUNK):
+        x_copy(j, layer, size).wait_recv()
         par = layer % 2
-        value = (table[near(j), :] + table[arrived(j, layer), :]).astype(BF16)
+        mine = rows_of(row, j, size)
+        here = rows_of(0, j, size)
+        value = (table[near(j, size), :] + table[arrived(j, layer, size), :]).astype(BF16)
         if layer < NUM_LAYERS:
-            panel[par, rows_of(row, j), :] = value
+            panel[par, mine, :] = value
 
             @pl.when(j % GROUP == GROUP - 1)
             def _():
                 ag_copy("x", j // GROUP, layer).start()
                 ag_copy("mate", j // GROUP, layer).start()
         else:
-            total = ei_ref[chunk_rows(j), :].astype(F32) + panel[1, rows_of(row, j), :].astype(F32)
-            total = total + panel[0, rows_of(row, j), :].astype(F32)
+            total = ei_ref[here, :].astype(F32) + panel[1, mine, :].astype(F32)
+            total = total + panel[0, mine, :].astype(F32)
             total = total + value.astype(F32)
             final = (total / (NUM_LAYERS + 1)).astype(BF16)
-            panel[1, rows_of(row, j), :] = final
-            outi_ref[chunk_rows(j), :] = final
-            table[near(j), :] = final.astype(F32)
-            fin_copy("col", j).start()
-            fin_copy("mate", j).start()
+            panel[1, mine, :] = final
+            outi_ref[here, :] = final
+            table[near(j, size), :] = final.astype(F32)
+            fin_copy("col", j, size).start()
+            fin_copy("mate", j, size).start()
 
     def gather_items(layer):
         for g in range(n_chunk // GROUP):
@@ -488,7 +496,7 @@
                 core_copy(slot, 0).wait_send()
         else:
             loop(0, n_chunk, functools.partial(item_send_step, layer=layer))
-            add_mate(n_chunk - 1, layer)
+            add_mate(n_chunk - 1, layer, halves if layer == NUM_LAYERS else None)
         if layer == 1:
             ag0_d.wait()
             ag0_f.wait()
@@ -538,9 +546,16 @@
     loop(n_chunk // 2, 3 * n_chunk // 4, last_step)
     gather_users()
     swap_users()
-    loop(3 * n_chunk // 4, n_chunk, last_step)
-    loop(n_chunk - LAG, n_chunk, fin_near)
-    loop(n_chunk - LAG - 2, n_chunk, fin_fwd)
+    last = n_chunk - 1
+    loop(3 * n_chunk // 4, last, last_step)
+    for j, size in halves:
+        finish_item(j, NUM_LAYERS, size)
+    loop(last - LAG, last, fin_near)
+    for j, size in halves:
+        fin_near(j, size)
+    loop(last - LAG - 2, last, fin_fwd)
+    for j, size in halves:
+        fin_fwd(j, size)
     for k in (1, 2):
         lo, hi = (k - 1) * share // 2, k * share // 2
         pick(table, 0, 1, yflat, lo, hi)
@@ -656,7 +671,7 @@
             one, dma((2, n_group)),
             one, dma((2, n_group)),
             one, dma((2, n_group)),
-            dma((3,)), dma((3, n_chunk)),
+            dma((3,)), dma((3, n_chunk)), dma((4,)),
             one, one,
         ],
         compiler_params=pltpu.CompilerParams(collective_id=0, has_side_effects=True,

time: 227 us -> 227 us (level)
  no operation moved by 1% of the time
where the time goes in v9:
time: 227 us; the launch traced here: 226 us
  Pallas kernels  226 us (100%)
    pallas_call x1, Pallas kernels, propagate(): pl.pallas_call(prop_kernel, name='propagate', out_shape=(vmem((own_u, dim...  225 us

profile of v9, /device:TPU:0, one launch (start us, length us, event | category | flops | bytes accessed | tf_op | source)
XLA Modules:
  0.0 226.4 jit_solution(7837733253550707839)
XLA Ops:
  0.6 224.7 %propagate.1 = (bf16[512,128]{1,0:T(8,128)(2,1)S(1)}, bf16[4096,128]{1,0:T(8,128)(2,1)S(1)}, f32[1,4096]{1,0:T(1,128)S(1)}) custom-call(s32[1024,16384]{1,0:T(8,128)} %mask_hbm.1, bf16[512,128]{1,0:T(8,128)(2,1)} %eu_hbm.1, bf16[4096,128]{1,0:T(8,128)(2,1)} %ei_hbm.1, s32[3,4096]{1,0:T(4,128)} %bitcast.2), custom_call_target="tpu_custom_call" | custom-call | tf_op jit(solution)/shard_map/propagate/pallas_call | solution.py:636
  225.4 1.1 hand_out.1

commit v10 on v9

--- a/solution.py
+++ b/solution.py
@@ -453,10 +453,13 @@
     def out_rows(lo, size):
         return pl.ds(pl.multiple_of(far * own_i + lo, size), size)
 
+    piece = share // GROUP
+
     def pick_copy(k):
-        lo, size = ((0, 2 * share), (2 * share, share // 2), (5 * share // 2, share // 2))[k]
+        lo, size = (2 * share + (k - 1) * piece, piece) if k else (0, 2 * share)
+        pool, at = (agx_r, k - 1) if k else (agf_r, 0)
         return remote(panel.at[0, out_rows(lo, size)], pick_in.at[pl.ds(lo, size)],
-                      agx_r.at[0, k], agx_r.at[1, k], to_far)
+                      pool.at[0, at], pool.at[1, at], to_far)
 
     def thirds(k):
         return pl.ds(k * share, share)
@@ -556,12 +559,12 @@
     loop(last - LAG - 2, last, fin_fwd)
     for j, size in halves:
         fin_fwd(j, size)
-    for k in (1, 2):
-        lo, hi = (k - 1) * share // 2, k * share // 2
+    for k in range(1, GROUP + 1):
+        lo, hi = (k - 1) * piece, k * piece
         pick(table, 0, 1, yflat, lo, hi)
         pick(table, 0, 2, yflat, lo, hi)
         diff = yflat[share + lo:share + hi, :] - yflat[2 * share + lo:2 * share + hi, :]
-        panel[0, out_rows(2 * share + lo, share // 2), :] = jnp.where(mixed[lo:hi, :] > 0.5, diff, 0.0).astype(BF16)
+        panel[0, out_rows(2 * share + lo, piece), :] = jnp.where(mixed[lo:hi, :] > 0.5, diff, 0.0).astype(BF16)
         pick_copy(k).start()
     pick(table, 1, 1, drecv)
     pick(table, 1, 2, drecv)
@@ -577,15 +580,15 @@
     dots[:, pl.ds(pl.multiple_of(base + share, share), share)] = score(e_far, diff)
     e_own = drecv[thirds(0), :] + pick_in[thirds(0), :].astype(F32)
     diff = drecv[thirds(1), :] - drecv[thirds(2), :]
-    pick_copy(1).wait_recv()
-    pick_copy(2).wait_recv()
+    for k in range(1, GROUP + 1):
+        pick_copy(k).wait_recv()
     diff = diff + pick_in[thirds(2), :].astype(F32)
     dots[:, pl.ds(pl.multiple_of(base, share), share)] = score(e_own, diff)
     mine = pl.ds(pl.multiple_of(base, 2 * share), 2 * share)
     for target in peers:
         remote(dots.at[:, mine], dots.at[:, mine], loss_s.at[0], loss_r.at[0], target).start()
 
-    for k in range(3):
+    for k in range(GROUP + 1):
         pick_copy(k).wait_send()
     for k, kind in enumerate(("col", "mate", "fwd")):
         fu_copy(kind).wait_send()

time: 227 us -> 226 us (level)
  no operation moved by 1% of the time
where the time goes in v10:
time: 226 us
  Pallas kernels  225 us (100%)
    pallas_call x1, Pallas kernels, propagate(): pl.pallas_call(prop_kernel, name='propagate', out_shape=(vmem((own_u, dim...  224 us

profile of v10, /device:TPU:0, one launch (start us, length us, event | category | flops | bytes accessed | tf_op | source)
XLA Modules:
  0.0 226.1 jit_solution(8645838050471269547)
XLA Ops:
  0.6 224.4 %propagate.1 = (bf16[512,128]{1,0:T(8,128)(2,1)S(1)}, bf16[4096,128]{1,0:T(8,128)(2,1)S(1)}, f32[1,4096]{1,0:T(1,128)S(1)}) custom-call(s32[1024,16384]{1,0:T(8,128)} %mask_hbm.1, bf16[512,128]{1,0:T(8,128)(2,1)} %eu_hbm.1, bf16[4096,128]{1,0:T(8,128)(2,1)} %ei_hbm.1, s32[3,4096]{1,0:T(4,128)} %bitcast.2), custom_call_target="tpu_custom_call" | custom-call | tf_op jit(solution)/shard_map/propagate/pallas_call | solution.py:639
  225.0 1.1 hand_out.1
